TPU v7x, 256 devices: a whole 4x4x8 slice. The times are simulated.
256 devices in a mesh: grp: 4 (over x), row: 64 (over y, z, core).
Axes of the slice: x: 4, y: 4, z: 8, core: 2. Of those that a mesh axis runs over, the one named last changes fastest.
Arguments:
- krylov_basis: bfloat16 [300, 4096, 512], P(None, 'row', 'grp'), may hold values from -30 to 30
- krylov_image: bfloat16 [300, 4096, 512], P(None, 'row', 'grp'), may hold values from -30 to 30
- tridiag_vectors: bfloat16 [300, 32], P(None, 'grp'), may hold values from -0.375 to 0.375
- ritz_values: bfloat16 [32], P('grp'), may hold values from -3 to 3
Outputs:
- ritz_vectors: float32 [32, 4096, 512], P('grp', 'row')
- ritz_residuals: float32 [32, 4096, 512], P('grp', 'row')
- residual_norms: float32 [32], P('grp')
All inputs are finite; a program needn't handle non-finite values.
Results may differ from a plain program's by a relative error of at most 0.0003.
Values may be sent and summed in bfloat16 or wider, within the bound.
No kernel may reach another device: no remote copies, remote signals or barrier semaphores. Data moves between devices by JAX's collectives and lax.ppermute only.
A program may use at most 64 MiB of HBM per device.

v0:
```python
import jax
import jax.numpy as jnp
from jax import lax
from jax.sharding import PartitionSpec as P


def turned_gather(arrays, axis, dims):
    turned = [jnp.moveaxis(a, dim, 0) for a, dim in zip(arrays, dims)]
    both = jnp.concatenate([t.reshape(len(t), -1) for t in turned], axis=1)
    out, at, done = (lax.all_gather(both, axis, axis=0, tiled=True), 0, [])
    for t, dim in zip(turned, dims):
        section = out[:, at : at + t[0].size].reshape(-1, *t.shape[1:])
        done.append(jnp.moveaxis(section, 0, dim))
        at += t[0].size
    return tuple(done)


def side_by_side(arrays, axis, split_dim, concat_dim, along):
    both = jnp.concatenate(arrays, axis=along)
    out, at, done = (
        lax.all_to_all(both, axis, split_axis=split_dim, concat_axis=concat_dim, tiled=True),
        0,
        [],
    )
    for a in arrays:
        done.append(lax.slice_in_dim(out, at, at + a.shape[along], axis=along))
        at += a.shape[along]
    return tuple(done)


def sent_to_all(value, axis):
    copies = jnp.broadcast_to(value, (lax.axis_size(axis), *value.shape))
    return lax.all_to_all(copies, axis, split_axis=0, concat_axis=0, tiled=True)


def of_everyone(value, axis):
    return sent_to_all(value, axis).sum(axis=0)


def packed_total(arrays, axis):
    line, at, done = (jnp.concatenate([a.reshape(-1) for a in arrays]), 0, [])
    so_far = of_everyone(line, axis)
    for a in arrays:
        done.append(so_far[at : at + a.size].reshape(a.shape))
        at += a.size
    return tuple(done)


def project(coef_cols, field_block):
    krylov_len = field_block.shape[0]
    flat_field = field_block.reshape(krylov_len, -1)
    result = lax.dot_general(
        coef_cols, flat_field, (((0,), (0,)), ((), ())), preferred_element_type=jnp.float32
    )
    return result.reshape(coef_cols.shape[1], field_block.shape[1], field_block.shape[2])


def column_pair(coef_cols, shift_values, basis_block, image_block):
    ritz_cols = project(coef_cols, basis_block)
    applied = project(coef_cols, image_block)
    resid_cols = applied - shift_values[:, None, None] * ritz_cols
    return (ritz_cols, resid_cols)


def squares_of(ritz_cols, resid_cols):
    return (
        jnp.sum(ritz_cols * ritz_cols, axis=(1, 2)),
        jnp.sum(resid_cols * resid_cols, axis=(1, 2)),
    )


def finish(ritz_cols, resid_cols, ritz_squares, resid_squares, rows_total):
    ritz_squares = ritz_squares + 1.0
    factor = jnp.sqrt(rows_total / ritz_squares)
    return (
        ritz_cols * factor[:, None, None],
        resid_cols * factor[:, None, None],
        jnp.sqrt(resid_squares / ritz_squares),
    )


def body(krylov_basis, krylov_image, tridiag_vectors, ritz_values):
    groups = lax.axis_size("grp")
    outer_dev = krylov_basis.shape[1]
    inner_dev = krylov_basis.shape[2]
    rows_total = float(outer_dev * inner_dev * groups * lax.axis_size("row"))
    all_coefs, all_values = turned_gather((tridiag_vectors, ritz_values), "grp", (1, 0))
    ritz_cols, resid_cols = column_pair(
        all_coefs, all_values.astype(jnp.float32), krylov_basis, krylov_image
    )
    owned_ritz, owned_resid = side_by_side((ritz_cols, resid_cols), "grp", 0, 2, 1)
    ritz_part, resid_part = squares_of(owned_ritz, owned_resid)
    ritz_squares, resid_squares = packed_total((ritz_part, resid_part), "row")
    return finish(owned_ritz, owned_resid, ritz_squares, resid_squares, rows_total)


def solution(mesh):
    placed = (P(None, "row", "grp"), P(None, "row", "grp"), P(None, "grp"), P("grp"))
    return jax.shard_map(
        body,
        mesh=mesh,
        in_specs=placed,
        out_specs=(P("grp", "row", None), P("grp", "row", None), P("grp")),
        check_vma=False,
    )
```

profile of v0, /device:TPU:1, one launch (start us, length us, event | category | flops | bytes accessed | tf_op | source)
XLA Modules:
  0.0 79.1 jit_solution(9452588244117255609)
XLA Ops:
  0.6 0.7 copy.23
  1.4 0.8 pad_maximum_fusion.1
  2.1 10.2 %all_gather.3 = bf16[32,301]{1,0:T(8,128)(2,1)S(1)} all-gather(bf16[8,301]{1,0:T(8,128)(2,1)S(1)} %pad_maximum_fusion.1), channel_id=1, replica_groups=mesh['grp'=4,'row'=64] {'grp'}, dimensions={0}, use_global_device_ids=true | all-gather | bytes 24080 | tf_op jit(solution)/shard_map/all_gather | solution.py:10
  12.4 0.2 convert_reduce_fusion
  12.5 3.5 %slice_bitcast_fusion.1 = bf16[64,128,300]{1,0,2:T(8,128)(2,1)S(1)} fusion(bf16[300,64,128]{2,1,0:T(8,128)(2,1)} %param.4), kind=kLoop, calls=%fused_computation.5 | loop fusion | bytes 9830400 | tf_op jit(solution)/shard_map/dot_general | solution.py:52
  16.1 0.0 copy-start
  16.1 3.1 %fusion.2 = f32[32,64,128]{2,0,1:T(8,128)S(1)} fusion(bf16[64,128,300]{1,0,2:T(8,128)(2,1)S(1)} %slice_bitcast_fusion.1, bf16[32,301]{1,0:T(8,128)(2,1)S(1)} %all_gather.3), kind=kOutput, calls=%fused_computation.2 | convolution fusion | flops 157286400 | bytes 5983040 | tf_op jit(solution)/shard_map/dot_general | solution.py:52
  19.2 0.0 copy-done
  19.2 1.1 %slice_bitcast_fusion = bf16[64,128,300]{1,0,2:T(8,128)(2,1)S(1)} fusion(bf16[300,64,128]{2,1,0:T(8,128)(2,1)S(1)} %copy-done), kind=kLoop, calls=%fused_computation.4 | loop fusion | bytes 9830400 | tf_op jit(solution)/shard_map/dot_general | solution.py:52
  20.3 3.0 %fusion.4 = f32[32,64,128]{2,0,1:T(8,128)S(1)} fusion(bf16[64,128,300]{1,0,2:T(8,128)(2,1)S(1)} %slice_bitcast_fusion, f32[32,64,128]{2,0,1:T(8,128)S(1)} %fusion.2, f32[32]{0:T(128)S(1)} %convert_reduce_fusion, bf16[32,301]{1,0:T(8,128)(2,1)S(1)} %all_gather.3), kind=kOutput, calls=%fused_computation.8 | convolution fusion | flops 157810688 | bytes 7031744 | tf_op jit(solution)/shard_map/dot_general | solution.py:52
  23.4 0.2 pad_maximum_fusion
  23.5 1.2 %copy.26 = f32[32,128,128]{2,1,0:T(8,128)S(1)} copy(f32[32,128,128]{2,0,1:T(8,128)S(1)} %pad_maximum_fusion) | data formatting | bytes 4194304 | tf_op jit(solution)/shard_map/concatenate | solution.py:19
  24.8 25.1 %all_to_all.24 = f32[32,128,128]{2,1,0:T(8,128)S(1)} all-to-all(f32[32,128,128]{2,1,0:T(8,128)S(1)} %copy.26), channel_id=1, replica_groups=mesh['grp'=4,'row'=64] {'grp'}, dimensions={0} | all-to-all | bytes 4194304 | tf_op jit(solution)/shard_map/all_to_all | solution.py:21
  49.9 0.3 copy.44
  50.1 0.3 multiply_reduce_fusion.1
  50.4 0.1 pad_maximum_fusion.2
  50.5 26.2 %all_to_all.25 = f32[64,1,16]{2,1,0:T(1,128)S(1)} all-to-all(f32[64,1,16]{2,1,0:T(1,128)S(1)} %broadcast_in_dim.2), channel_id=1, replica_groups=mesh['grp'=4,'row'=64] {'row'}, dimensions={0} | all-to-all | bytes 8192 | tf_op jit(solution)/shard_map/all_to_all | solution.py:33
  76.7 0.1 reduce_sum.29
  76.8 0.6 fusion.7
  77.4 1.8 %slice_multiply_fusion = (f32[8,64,512]{2,1,0:T(8,128)}, f32[8,64,512]{2,1,0:T(8,128)}) fusion(f32[8,128,512]{2,1,0:T(8,128)S(1)} %bitcast.38, f32[8]{0:T(128)S(1)} %get-tuple-element.8), kind=kLoop, calls=%fused_computation.11 | loop fusion | flops 524288 | bytes 4194336 | tf_op jit(solution)/shard_map/mul | solution.py:77
  (1 shorter events, 0.0 us)
Async XLA Ops:
  16.1 3.1 %copy-start = (bf16[300,64,128]{2,1,0:T(8,128)(2,1)S(1)}, bf16[300,64,128]{2,1,0:T(8,128)(2,1)}, u32[]{:S(2)}) copy-start(bf16[300,64,128]{2,1,0:T(8,128)(2,1)} %param.5) | copy-start | bytes 14745604
where the time goes:
time: 79.4 us; the launch traced here: 79.1 us
  blocking collectives  61.5 us (77%)
  local copies, waits for them, and re-layouts  6.94 us (9%)
  matrix products  6.08 us (8%)
  other arithmetic  3.88 us (5%)
    all_to_all x1, blocking collectives, sent_to_all(): return lax.all_to_all(copies, axis, split_axis=0, concat_axis=0, tiled=True)  26.2 us
    all_to_all x1, blocking collectives, side_by_side(): lax.all_to_all(both, axis, split_axis=split_dim, concat_axis=concat_dim,...  25.1 us
    all_gather x1, blocking collectives, turned_gather(): out, at, done = (lax.all_gather(both, axis, axis=0, tiled=True), 0, [])  10.2 us
    dot_general x2, matrix products, project(): lax.dot_general(coef_cols, flat_field, (((0,), (0,)), ((), ())), preferre...  6.08 us
    dot_general x2, local copies, waits for them, and re-layouts, project(): lax.dot_general(coef_cols, flat_field, (((0,), (0,)), ((), ())), preferre...  4.69 us
    mul x1, other arithmetic, finish(): resid_cols * factor[:, None, None]  1.75 us

commit v1 on v0

v1 whole, which is shorter than its diff:
```python
import functools

import jax
import jax.numpy as jnp
from jax import lax
from jax.experimental import pallas as pl
from jax.experimental.pallas import tpu as pltpu
from jax.sharding import PartitionSpec as P

LANES = 128
SHIFT_AT = 384


def pack_kernel(coef_ref, value_ref, out_ref):
    cols, krylov = coef_ref.shape
    out_ref[...] = jnp.zeros_like(out_ref)
    out_ref[:, :krylov] = coef_ref[...]
    row = lax.broadcasted_iota(jnp.int32, (cols, cols), 0)
    lane = lax.broadcasted_iota(jnp.int32, (cols, cols), 1)
    values = jnp.broadcast_to(value_ref[...].astype(jnp.float32), (cols, cols))
    column = jnp.sum(jnp.where(row == lane, values, 0.0), axis=1, keepdims=True)
    out_ref[:, SHIFT_AT:] = jnp.broadcast_to(column, (cols, LANES)).astype(jnp.bfloat16)


def power_of_two(exponent, sign):
    out = jnp.ones(exponent.shape, jnp.float32)
    whole = exponent.astype(jnp.int32)
    for bit in range(7):
        out = out * jnp.where((whole & (1 << bit)) != 0, 2.0 ** (sign * (1 << bit)), 1.0)
    return out


def project_kernel(*refs, groups, per_step):
    coef_refs, (basis_ref, image_ref) = refs[:groups], refs[groups : groups + 2]
    own_ref = refs[groups + 2]
    chunk_refs = refs[groups + 3 : 2 * groups + 2]
    sum_refs = refs[2 * groups + 2 : 3 * groups + 2]
    held, squares, peaks = refs[3 * groups + 2 :]
    krylov = basis_ref.shape[0]
    cols = coef_refs[0].shape[0]
    wanted = groups * cols
    step = pl.program_id(0)

    @pl.when(step == 0)
    def _():
        squares[...] = jnp.zeros_like(squares)
        peaks[...] = jnp.zeros_like(peaks)

    coefs = jnp.concatenate([ref[:, :krylov].astype(jnp.float32) for ref in coef_refs])
    coefs = coefs.astype(jnp.bfloat16)
    shift = jnp.concatenate([ref[:, SHIFT_AT:].astype(jnp.float32) for ref in coef_refs])
    shift = jnp.concatenate([shift, shift], axis=1)
    basis = jnp.swapaxes(basis_ref[...], 0, 1)
    image = jnp.swapaxes(image_ref[...], 0, 1)
    for pair in range(0, per_step, 2):
        fields = []
        for field in (basis, image):
            both = jnp.concatenate([field[pair], field[pair + 1]], axis=1)
            fields.append(jnp.dot(coefs, both, preferred_element_type=jnp.float32))
        ritz, resid = fields[0], fields[1] - shift * fields[0]
        for at, value in ((0, ritz), (wanted, resid)):
            squares[at : at + wanted] += value * value
            peaks[at : at + wanted] = jnp.maximum(peaks[at : at + wanted], jnp.abs(value))
            for half in range(2):
                held[step * per_step + pair + half, at : at + wanted] = value[:, half * LANES : (half + 1) * LANES]

    @pl.when(step == pl.num_programs(0) - 1)
    def _():
        sums = jnp.sum(squares[...], axis=1, keepdims=True)
        row = lax.broadcasted_iota(jnp.int32, (cols, LANES), 0)
        lane = lax.broadcasted_iota(jnp.int32, (cols, LANES), 1)
        for s in range(groups):
            line = jnp.where(lane == row, sums[s * cols : (s + 1) * cols], 0.0)
            at = wanted + s * cols
            line = line + jnp.where(lane == row + cols, sums[at : at + cols], 0.0)
            sum_refs[s][...] = jnp.sum(line, axis=0, keepdims=True)
        peak = jnp.max(peaks[...], axis=1, keepdims=True)
        exponent = jnp.clip(jnp.floor(14.0 - jnp.log(peak) * 1.4426950408889634), 0.0, 100.0)
        exponent = jnp.broadcast_to(exponent, (2 * wanted, LANES))
        scale = power_of_two(exponent, 1)
        outer = held.shape[0]
        for s in range(groups):
            for which in range(2):
                at = which * wanted + s * cols
                block = jnp.swapaxes(held[:, at : at + cols, :], 0, 1)
                if s == 0:
                    own_ref[which * cols : (which + 1) * cols] = block
                else:
                    block = block * scale[at : at + cols][:, None, :]
                    ref = chunk_refs[s - 1]
                    ref[pl.ds(which * cols * outer, cols * outer), :] = block.reshape(cols * outer, LANES)
                    ref[pl.ds(2 * cols * outer + which * cols, cols), :] = exponent[at : at + cols]


def finish_kernel(*refs, groups, rows_total):
    own_ref, chunk_refs, total_ref = refs[0], refs[1:groups], refs[groups]
    outs, norm_ref = refs[groups + 1 : groups + 3], refs[groups + 3]
    double, outer, _ = own_ref.shape
    cols = double // 2
    total = jnp.sum(total_ref[...], axis=0, keepdims=True)
    row = lax.broadcasted_iota(jnp.int32, (cols, LANES), 0)
    lane = lax.broadcasted_iota(jnp.int32, (cols, LANES), 1)
    ritz = jnp.sum(jnp.where(lane == row, total, 0.0), axis=1, keepdims=True) + 1.0
    resid = jnp.sum(jnp.where(lane == row + cols, total, 0.0), axis=1, keepdims=True)
    factor = jnp.broadcast_to(jnp.sqrt(rows_total / ritz), (cols, LANES))
    norms = jnp.sqrt(resid / ritz)
    norm_ref[...] = jnp.sum(jnp.where(lane == row, norms, 0.0), axis=0, keepdims=True)
    me = lax.axis_index("grp")
    for s in range(groups):
        source = lax.rem(me + groups - s, groups)
        at = pl.ds(pl.multiple_of(source * LANES, LANES), LANES)
        for which in range(2):
            if s == 0:
                block = own_ref[which * cols : (which + 1) * cols]
                gain = factor
            else:
                ref = chunk_refs[s - 1]
                block = ref[pl.ds(which * cols * outer, cols * outer), :].reshape(cols, outer, LANES)
                exponent = ref[pl.ds(2 * cols * outer + which * cols, cols), :]
                gain = factor * power_of_two(exponent, -1)
            outs[which][:, :, at] = block * gain[:, None, :]


def shifted(value, s, groups):
    return lax.ppermute(value, "grp", [(i, (i + s) % groups) for i in range(groups)])


def everyone(value, axis):
    size = lax.axis_size(axis)
    copies = jnp.broadcast_to(value[None], (size, *value.shape))
    return lax.all_to_all(copies, axis, split_axis=0, concat_axis=0, tiled=True)


def body(krylov_basis, krylov_image, tridiag_vectors, ritz_values):
    groups = lax.axis_size("grp")
    krylov, outer, inner = krylov_basis.shape
    cols = tridiag_vectors.shape[1]
    rows_total = float(outer * inner * groups * lax.axis_size("row"))
    f32 = jnp.float32
    own_coefs = pl.pallas_call(
        pack_kernel, out_shape=jax.ShapeDtypeStruct((cols, SHIFT_AT + LANES), jnp.bfloat16), name="pack"
    )(tridiag_vectors.T, ritz_values[None, :])
    coefs = [own_coefs] + [shifted(own_coefs, groups - s, groups) for s in range(1, groups)]

    per_step = 16
    whole = lambda shape: pl.BlockSpec(shape, lambda j: (0,) * len(shape))
    field = pl.BlockSpec((krylov, per_step, inner), lambda j: (0, j, 0))
    chunk = (2 * cols * (outer + 1), LANES)
    shapes = [(2 * cols, outer, LANES)] + [chunk] * (groups - 1) + [(1, LANES)] * groups
    outs = pl.pallas_call(
        functools.partial(project_kernel, groups=groups, per_step=per_step),
        grid=(outer // per_step,),
        in_specs=[whole(own_coefs.shape)] * groups + [field] * 2,
        out_specs=[whole(shape) for shape in shapes],
        out_shape=[jax.ShapeDtypeStruct(shape, f32) for shape in shapes],
        scratch_shapes=[
            pltpu.VMEM((outer, 2 * groups * cols, LANES), f32),
            pltpu.VMEM((2 * groups * cols, 2 * LANES), f32),
            pltpu.VMEM((2 * groups * cols, 2 * LANES), f32),
        ],
        name="project",
    )(*coefs, krylov_basis, krylov_image)
    own, chunks, sums = outs[0], outs[1:groups], outs[groups:]
    total = sums[0] + sum(shifted(sums[s], s, groups) for s in range(1, groups))
    chunks = [shifted(c.astype(jnp.float16), s + 1, groups).astype(f32) for s, c in enumerate(chunks)]
    totals = everyone(total, "row").reshape(-1, LANES)
    ritz, resid, norms = pl.pallas_call(
        functools.partial(finish_kernel, groups=groups, rows_total=rows_total),
        out_shape=[jax.ShapeDtypeStruct((cols, outer, groups * inner), f32)] * 2
        + [jax.ShapeDtypeStruct((1, LANES), f32)],
        name="finish",
    )(own, *chunks, totals)
    return ritz, resid, norms[0, :cols]


def solution(mesh):
    placed = (P(None, "row", "grp"), P(None, "row", "grp"), P(None, "grp"), P("grp"))
    return jax.shard_map(
        body,
        mesh=mesh,
        in_specs=placed,
        out_specs=(P("grp", "row", None), P("grp", "row", None), P("grp")),
        check_vma=False,
    )
```

time: 79.4 us -> 59.4 us (0.75)
  blocking collectives: 61.5 us -> 0 us
  starting transfers between devices: 0 us -> 27.7 us
  Pallas kernels: 0 us -> 12.6 us
  waiting for transfers between devices: 0 us -> 8.55 us
  matrix products: 6.08 us -> 0 us
  local copies, waits for them, and re-layouts: 6.94 us -> 3.01 us
  other arithmetic: 3.88 us -> 6.44 us
    all_to_all x2 -> x0, blocking collectives: 51.3 us -> none  [the longest x1 26.2 us: sent_to_all(): return lax.all_to_all(copies, axis, split_axis=0, concat_axis=0, tiled=True)]
    all_to_all x0 -> x1, starting transfers between devices: none -> 15.4 us  [everyone(): return lax.all_to_all(copies, axis, split_axis=0, concat_axis=0, tiled=True)]
    pallas_call x0 -> x3, Pallas kernels: none -> 12.6 us  [the longest x1 8.14 us: body(): pl.pallas_call(functools.partial(project_kernel, groups=groups, per_step=...]
    ppermute x0 -> x9, starting transfers between devices: none -> 12.3 us  [shifted(): lax.ppermute(value, 'grp', [(i, (i + s) % groups) for i in range(groups)])]
    all_gather x1 -> x0, blocking collectives: 10.2 us -> none  [turned_gather(): out, at, done = (lax.all_gather(both, axis, axis=0, tiled=True), 0, [])]
    all_to_all x0 -> x1, waiting for transfers between devices: none -> 6.69 us  [everyone(): return lax.all_to_all(copies, axis, split_axis=0, concat_axis=0, tiled=True)]
    dot_general x2 -> x0, matrix products: 6.08 us -> none  [project(): lax.dot_general(coef_cols, flat_field, (((0,), (0,)), ((), ())), preferre...]
    convert_element_type x1 -> x6, other arithmetic: 0.18 us -> 5.78 us  [the longest x3 3.25 us: body(): c.astype(jnp.float16)]
  transfers between devices with their start and end apart: 0 -> 10, of which waited for: 0 -> 3; matrix products, arithmetic and copies ran while one was open for 0% -> 12% of each run, Pallas kernels for 0% -> 0%
where the time goes in v1:
time: 59.4 us; the launch traced here: 59 us
  starting transfers between devices  27.7 us (47%)
  Pallas kernels  12.6 us (21%)
  waiting for transfers between devices  8.55 us (14%)
  other arithmetic  6.44 us (11%)
  local copies, waits for them, and re-layouts  3.01 us (5%)
  between operations  0.69 us (1%)
    all_to_all x1, starting transfers between devices, everyone(): return lax.all_to_all(copies, axis, split_axis=0, concat_axis=0, tiled=True)  15.4 us
    ppermute x9, starting transfers between devices, shifted(): lax.ppermute(value, 'grp', [(i, (i + s) % groups) for i in range(groups)])  12.3 us
    pallas_call x1, Pallas kernels, body(): pl.pallas_call(functools.partial(project_kernel, groups=groups, per_step=...  8.14 us
    all_to_all x1, waiting for transfers between devices, everyone(): return lax.all_to_all(copies, axis, split_axis=0, concat_axis=0, tiled=True)  6.69 us
    convert_element_type x3, other arithmetic, body(): c.astype(jnp.float16)  3.25 us
    pallas_call x1, Pallas kernels, body(): pl.pallas_call(functools.partial(finish_kernel, groups=groups, rows_total...  3.09 us
    convert_element_type x3, other arithmetic, body(): shifted(c.astype(jnp.float16), s + 1, groups).astype(f32)  2.53 us
    ppermute x9, waiting for transfers between devices, shifted(): lax.ppermute(value, 'grp', [(i, (i + s) % groups) for i in range(groups)])  1.86 us
  transfers between devices with their start and end apart: 10, of which 3 were waited for; matrix products, arithmetic and copies ran while one was open for 12% of the time, Pallas kernels for 0%

profile of v1, /device:TPU:1, one launch (start us, length us, event | category | flops | bytes accessed | tf_op | source)
XLA Modules:
  0.0 59.0 jit_solution(6366024762759856505)
XLA Ops:
  0.6 1.4 %pack.1.refs_0_ = bf16[8,512]{1,0:T(8,128)(2,1)} custom-call(bf16[8,300]{1,0:T(8,128)(2,1)} %bitcast.8, bf16[1,8]{1,0:T(2,128)(2,1)} %bitcast.9), custom_call_target="tpu_custom_call" | custom-call | tf_op jit(solution)/shard_map/pack/pallas_call | solution.py:140
  2.0 2.0 %collective-permute-start.2 = (bf16[8,512]{1,0:T(8,128)(2,1)}, bf16[8,512]{1,0:T(8,128)(2,1)S(1)}, u32[]{:S(2)}, u32[]{:S(2)}) collective-permute-start(bf16[8,512]{1,0:T(8,128)(2,1)} %pack.1.refs_0_), channel_id=1, source_target_pairs={{0,64},{64,128},{128,192},{192,0},{1,65},{65,129},{129,193},{193,1... | collective-permute-start | bytes 24584 | tf_op jit(solution)/shard_map/ppermute | solution.py:125
  4.0 2.5 %collective-permute-start.1 = (bf16[8,512]{1,0:T(8,128)(2,1)}, bf16[8,512]{1,0:T(8,128)(2,1)S(1)}, u32[]{:S(2)}, u32[]{:S(2)}) collective-permute-start(bf16[8,512]{1,0:T(8,128)(2,1)} %pack.1.refs_0_), channel_id=1, source_target_pairs={{0,128},{64,192},{128,0},{192,64},{1,129},{65,193},{129,1},{193,65... | collective-permute-start | bytes 24584 | tf_op jit(solution)/shard_map/ppermute | solution.py:125
  6.5 1.2 %collective-permute-start = (bf16[8,512]{1,0:T(8,128)(2,1)}, bf16[8,512]{1,0:T(8,128)(2,1)S(1)}, u32[]{:S(2)}, u32[]{:S(2)}) collective-permute-start(bf16[8,512]{1,0:T(8,128)(2,1)} %pack.1.refs_0_), channel_id=1, source_target_pairs={{0,192},{64,0},{128,64},{192,128},{1,193},{65,1},{129,65},{193,129... | collective-permute-start | bytes 24584 | tf_op jit(solution)/shard_map/ppermute | solution.py:125
  7.6 0.6 %collective-permute-done.1.refs_2_ = bf16[8,512]{1,0:T(8,128)(2,1)S(1)} collective-permute-done((bf16[8,512]{1,0:T(8,128)(2,1)}, bf16[8,512]{1,0:T(8,128)(2,1)S(1)}, u32[]{:S(2)}, u32[]{:S(2)}) %collective-permute-start.1) | collective-permute-done | bytes 8224 | tf_op jit(solution)/shard_map/ppermute | solution.py:125
  8.2 1.2 %collective-permute-done.refs_1_ = bf16[8,512]{1,0:T(8,128)(2,1)S(1)} collective-permute-done((bf16[8,512]{1,0:T(8,128)(2,1)}, bf16[8,512]{1,0:T(8,128)(2,1)S(1)}, u32[]{:S(2)}, u32[]{:S(2)}) %collective-permute-start) | collective-permute-done | bytes 8224 | tf_op jit(solution)/shard_map/ppermute | solution.py:125
  10.1 8.1 %project.1 = (f32[16,64,128]{2,1,0:T(8,128)}, f32[1040,128]{1,0:T(8,128)}, f32[1040,128]{1,0:T(8,128)}, f32[1040,128]{1,0:T(8,128)}, f32[1,128]{1,0:T(1,128)}, /...) custom-call(bf16[8,512]{1,0:T(8,128)(2,1)} %pack.1.refs_0_, bf16[8,512]{1,0:T(8,128)(2,1)} %copy-done.3, ...), custom_call_target="tpu_custom_call" | custom-call | tf_op jit(solution)/shard_map/project/pallas_call | solution.py:150
  18.2 0.6 %collective-permute-start.6 = (f32[1,128]{1,0:T(1,128)}, f32[1,128]{1,0:T(1,128)S(1)}, u32[]{:S(2)}, u32[]{:S(2)}) collective-permute-start(f32[1,128]{1,0:T(1,128)} %get-tuple-element.19), channel_id=1, source_target_pairs={{0,64},{64,128},{128,192},{192,0},{1,65},{65,129},{129,193},{193,1... | collective-permute-start | bytes 1544 | tf_op jit(solution)/shard_map/ppermute | solution.py:125
  18.9 2.7 %collective-permute-start.7 = (f32[1,128]{1,0:T(1,128)}, f32[1,128]{1,0:T(1,128)S(1)}, u32[]{:S(2)}, u32[]{:S(2)}) collective-permute-start(f32[1,128]{1,0:T(1,128)} %get-tuple-element.20), channel_id=1, source_target_pairs={{0,128},{64,192},{128,0},{192,64},{1,129},{65,193},{129,1},{193,65... | collective-permute-start | bytes 1544 | tf_op jit(solution)/shard_map/ppermute | solution.py:125
  21.6 0.6 %collective-permute-start.8 = (f32[1,128]{1,0:T(1,128)}, f32[1,128]{1,0:T(1,128)S(1)}, u32[]{:S(2)}, u32[]{:S(2)}) collective-permute-start(f32[1,128]{1,0:T(1,128)} %get-tuple-element.21), channel_id=1, source_target_pairs={{0,192},{64,0},{128,64},{192,128},{1,193},{65,1},{129,65},{193,129... | collective-permute-start | bytes 1544 | tf_op jit(solution)/shard_map/ppermute | solution.py:125
  22.2 1.1 %convert_element_type.18 = f16[1040,128]{1,0:T(8,128)(2,1)S(1)} convert(f32[1040,128]{1,0:T(8,128)} %get-tuple-element.15) | non-fusion elementwise | flops 133120 | bytes 798720 | tf_op jit(solution)/shard_map/convert_element_type | solution.py:165
  23.3 1.1 %convert_element_type.20 = f16[1040,128]{1,0:T(8,128)(2,1)S(1)} convert(f32[1040,128]{1,0:T(8,128)} %get-tuple-element.16) | non-fusion elementwise | flops 133120 | bytes 798720 | tf_op jit(solution)/shard_map/convert_element_type | solution.py:165
  24.3 1.1 %convert_element_type.22 = f16[1040,128]{1,0:T(8,128)(2,1)S(1)} convert(f32[1040,128]{1,0:T(8,128)} %get-tuple-element.17) | non-fusion elementwise | flops 133120 | bytes 798720 | tf_op jit(solution)/shard_map/convert_element_type | solution.py:165
  25.5 2.6 %collective-permute-start.4 = (f16[1040,128]{1,0:T(8,128)(2,1)S(1)}, f16[1040,128]{1,0:T(8,128)(2,1)S(1)}, u32[]{:S(2)}, u32[]{:S(2)}) collective-permute-start(f16[1040,128]{1,0:T(8,128)(2,1)S(1)} %convert_element_type.20), channel_id=1, source_target_pairs={{0,128},{64,192},{128,0},{192,64},{1,129},{65,193},{129,1},{193,65... | collective-permute-start | bytes 798728 | tf_op jit(solution)/shard_map/ppermute | solution.py:125
  28.2 0.7 %add_bitcast_fusion = f32[128]{0:T(128)S(1)} fusion(f32[1,128]{1,0:T(1,128)} %get-tuple-element.18, f32[1,128]{1,0:T(1,128)S(1)} %collective-permute-done.8, f32[1,128]{1,0:T(1,128)S(1)} %collective-permute-done.6, f32[1,128]{1,0:T(1,128)S(1)} %collective-permute-done.7), kind=kLoop, calls=%fused_computation.1 | loop fusion | flops 384 | bytes 2560 | tf_op jit(solution)/shard_map/broadcast_in_dim | solution.py:130
  28.8 0.6 %broadcast_in_dim.13 = f32[64,1,128]{2,1,0:T(1,128)} broadcast(f32[128]{0:T(128)S(1)} %add_bitcast_fusion), dimensions={2} | broadcast | bytes 33280 | tf_op jit(solution)/shard_map/broadcast_in_dim | solution.py:130
  29.5 15.4 %all-to-all-start = ((f32[64,1,128]{2,1,0:T(1,128)}), f32[64,1,128]{2,1,0:T(1,128)S(1)}, u32[]{:S(2)}, u32[]{:S(2)}) async-start(f32[64,1,128]{2,1,0:T(1,128)} %broadcast_in_dim.13), calls=%async_computation | async-start | bytes 65536 | tf_op jit(solution)/shard_map/all_to_all | solution.py:131
  44.9 0.9 %convert_element_type.23.refs_3_ = f32[1040,128]{1,0:T(8,128)} convert(f16[1040,128]{1,0:T(8,128)(2,1)S(1)} %collective-permute-done.5) | non-fusion elementwise | flops 133120 | bytes 798720 | tf_op jit(solution)/shard_map/convert_element_type | solution.py:165
  45.8 0.8 %convert_element_type.21.refs_2_ = f32[1040,128]{1,0:T(8,128)} convert(f16[1040,128]{1,0:T(8,128)(2,1)S(1)} %collective-permute-done.4) | non-fusion elementwise | flops 133120 | bytes 798720 | tf_op jit(solution)/shard_map/convert_element_type | solution.py:165
  46.6 0.8 %convert_element_type.19.refs_1_ = f32[1040,128]{1,0:T(8,128)} convert(f16[1040,128]{1,0:T(8,128)(2,1)S(1)} %collective-permute-done.3) | non-fusion elementwise | flops 133120 | bytes 798720 | tf_op jit(solution)/shard_map/convert_element_type | solution.py:165
  47.5 6.7 %all-to-all-done = f32[64,1,128]{2,1,0:T(1,128)S(1)} async-done(((f32[64,1,128]{2,1,0:T(1,128)}), f32[64,1,128]{2,1,0:T(1,128)S(1)}, u32[]{:S(2)}, u32[]{:S(2)}) %all-to-all-start) | async-done | bytes 32800 | tf_op jit(solution)/shard_map/all_to_all | solution.py:131
  54.2 0.6 %copy-done = f32[64,1,128]{2,1,0:T(1,128)} copy-done((f32[64,1,128]{2,1,0:T(1,128)}, f32[64,1,128]{2,1,0:T(1,128)S(1)}, u32[]{:S(2)}) %copy-start) | copy-done | bytes 32792
  54.8 3.1 %finish.1 = (f32[8,64,512]{2,1,0:T(8,128)}, f32[8,64,512]{2,1,0:T(8,128)}, f32[1,128]{1,0:T(1,128)}) custom-call(f32[16,64,128]{2,1,0:T(8,128)} %get-tuple-element.14.refs_0_, f32[1040,128]{1,0:T(8,128)} %convert_element_type.19.refs_1_, f32[1040,128]{1,0:T(8,128)} %convert_element_type.21.refs_2_, f32[1040,128]{1,0:T(8,128)} %convert_element_type.23.refs_3_, ...), custom_call_target="tpu_custom_call" | custom-call | tf_op jit(solution)/shard_map/finish/pallas_call | solution.py:167
  57.8 1.2 %slice_bitcast_fusion = f32[8]{0:T(128)} fusion(f32[1,128]{1,0:T(1,128)} %get-tuple-element.24), kind=kLoop, calls=%fused_computation | loop fusion | bytes 64 | tf_op jit(solution)/shard_map/squeeze | solution.py:173
  (16 shorter events, 0.7 us)
Async XLA Ops:
  2.0 5.6 %collective-permute-start.2 = (bf16[8,512]{1,0:T(8,128)(2,1)}, bf16[8,512]{1,0:T(8,128)(2,1)S(1)}, u32[]{:S(2)}, u32[]{:S(2)}) collective-permute-start(bf16[8,512]{1,0:T(8,128)(2,1)} %pack.1.refs_0_), channel_id=1, source_target_pairs={{0,64},{64,128},{128,192},{192,0},{1,65},{65,129},{129,193},{193,1... | collective-permute-start | bytes 24584 | tf_op jit(solution)/shard_map/ppermute | solution.py:125
  4.0 4.2 %collective-permute-start.1 = (bf16[8,512]{1,0:T(8,128)(2,1)}, bf16[8,512]{1,0:T(8,128)(2,1)S(1)}, u32[]{:S(2)}, u32[]{:S(2)}) collective-permute-start(bf16[8,512]{1,0:T(8,128)(2,1)} %pack.1.refs_0_), channel_id=1, source_target_pairs={{0,128},{64,192},{128,0},{192,64},{1,129},{65,193},{129,1},{193,65... | collective-permute-start | bytes 24584 | tf_op jit(solution)/shard_map/ppermute | solution.py:125
  6.5 3.0 %collective-permute-start = (bf16[8,512]{1,0:T(8,128)(2,1)}, bf16[8,512]{1,0:T(8,128)(2,1)S(1)}, u32[]{:S(2)}, u32[]{:S(2)}) collective-permute-start(bf16[8,512]{1,0:T(8,128)(2,1)} %pack.1.refs_0_), channel_id=1, source_target_pairs={{0,192},{64,0},{128,64},{192,128},{1,193},{65,1},{129,65},{193,129... | collective-permute-start | bytes 24584 | tf_op jit(solution)/shard_map/ppermute | solution.py:125
  7.6 1.9 %copy-start.1 = (bf16[8,512]{1,0:T(8,128)(2,1)}, bf16[8,512]{1,0:T(8,128)(2,1)S(1)}, u32[]{:S(2)}) copy-start(bf16[8,512]{1,0:T(8,128)(2,1)S(1)} %collective-permute-done.2.refs_3_) | copy-start | bytes 24580
  8.2 1.2 %copy-start.2 = (bf16[8,512]{1,0:T(8,128)(2,1)}, bf16[8,512]{1,0:T(8,128)(2,1)S(1)}, u32[]{:S(2)}) copy-start(bf16[8,512]{1,0:T(8,128)(2,1)S(1)} %collective-permute-done.1.refs_2_) | copy-start | bytes 24580
  9.5 0.6 %copy-start.3 = (bf16[8,512]{1,0:T(8,128)(2,1)}, bf16[8,512]{1,0:T(8,128)(2,1)S(1)}, u32[]{:S(2)}) copy-start(bf16[8,512]{1,0:T(8,128)(2,1)S(1)} %collective-permute-done.refs_1_) | copy-start | bytes 24580
  18.2 9.9 %collective-permute-start.6 = (f32[1,128]{1,0:T(1,128)}, f32[1,128]{1,0:T(1,128)S(1)}, u32[]{:S(2)}, u32[]{:S(2)}) collective-permute-start(f32[1,128]{1,0:T(1,128)} %get-tuple-element.19), channel_id=1, source_target_pairs={{0,64},{64,128},{128,192},{192,0},{1,65},{65,129},{129,193},{193,1... | collective-permute-start | bytes 1544 | tf_op jit(solution)/shard_map/ppermute | solution.py:125
  18.9 9.3 %collective-permute-start.7 = (f32[1,128]{1,0:T(1,128)}, f32[1,128]{1,0:T(1,128)S(1)}, u32[]{:S(2)}, u32[]{:S(2)}) collective-permute-start(f32[1,128]{1,0:T(1,128)} %get-tuple-element.20), channel_id=1, source_target_pairs={{0,128},{64,192},{128,0},{192,64},{1,129},{65,193},{129,1},{193,65... | collective-permute-start | bytes 1544 | tf_op jit(solution)/shard_map/ppermute | solution.py:125
  21.6 6.6 %collective-permute-start.8 = (f32[1,128]{1,0:T(1,128)}, f32[1,128]{1,0:T(1,128)S(1)}, u32[]{:S(2)}, u32[]{:S(2)}) collective-permute-start(f32[1,128]{1,0:T(1,128)} %get-tuple-element.21), channel_id=1, source_target_pairs={{0,192},{64,0},{128,64},{192,128},{1,193},{65,1},{129,65},{193,129... | collective-permute-start | bytes 1544 | tf_op jit(solution)/shard_map/ppermute | solution.py:125
  25.4 19.5 %collective-permute-start.5 = (f16[1040,128]{1,0:T(8,128)(2,1)S(1)}, f16[1040,128]{1,0:T(8,128)(2,1)S(1)}, u32[]{:S(2)}, u32[]{:S(2)}) collective-permute-start(f16[1040,128]{1,0:T(8,128)(2,1)S(1)} %convert_element_type.22), channel_id=1, source_target_pairs={{0,192},{64,0},{128,64},{192,128},{1,193},{65,1},{129,65},{193,129... | collective-permute-start | bytes 798728 | tf_op jit(solution)/shard_map/ppermute | solution.py:125
  25.5 20.3 %collective-permute-start.4 = (f16[1040,128]{1,0:T(8,128)(2,1)S(1)}, f16[1040,128]{1,0:T(8,128)(2,1)S(1)}, u32[]{:S(2)}, u32[]{:S(2)}) collective-permute-start(f16[1040,128]{1,0:T(8,128)(2,1)S(1)} %convert_element_type.20), channel_id=1, source_target_pairs={{0,128},{64,192},{128,0},{192,64},{1,129},{65,193},{129,1},{193,65... | collective-permute-start | bytes 798728 | tf_op jit(solution)/shard_map/ppermute | solution.py:125
  28.2 18.5 %collective-permute-start.3 = (f16[1040,128]{1,0:T(8,128)(2,1)S(1)}, f16[1040,128]{1,0:T(8,128)(2,1)S(1)}, u32[]{:S(2)}, u32[]{:S(2)}) collective-permute-start(f16[1040,128]{1,0:T(8,128)(2,1)S(1)} %convert_element_type.18), channel_id=1, source_target_pairs={{0,64},{64,128},{128,192},{192,0},{1,65},{65,129},{129,193},{193,1... | collective-permute-start | bytes 798728 | tf_op jit(solution)/shard_map/ppermute | solution.py:125
  29.5 24.7 %all-to-all-start = ((f32[64,1,128]{2,1,0:T(1,128)}), f32[64,1,128]{2,1,0:T(1,128)S(1)}, u32[]{:S(2)}, u32[]{:S(2)}) async-start(f32[64,1,128]{2,1,0:T(1,128)} %broadcast_in_dim.13), calls=%async_computation | async-start | bytes 65536 | tf_op jit(solution)/shard_map/all_to_all | solution.py:131
  54.2 0.6 %copy-start = (f32[64,1,128]{2,1,0:T(1,128)}, f32[64,1,128]{2,1,0:T(1,128)S(1)}, u32[]{:S(2)}) copy-start(f32[64,1,128]{2,1,0:T(1,128)S(1)} %all-to-all-done) | copy-start | bytes 98308

commit v2 on v1

v2 whole, which is shorter than its diff:
```python
import functools

import jax
import jax.numpy as jnp
from jax import lax
from jax.experimental import pallas as pl
from jax.experimental.pallas import tpu as pltpu
from jax.sharding import PartitionSpec as P


LANES = 128
SHIFT_AT = 384


def pack_kernel(coef_hbm, value_hbm, out_ref, coef_ref, value_ref, arrived):
    cols, krylov = coef_ref.shape
    copies = [
        pltpu.make_async_copy(coef_hbm, coef_ref, arrived.at[0]),
        pltpu.make_async_copy(value_hbm, value_ref, arrived.at[1]),
    ]
    for copy in copies:
        copy.start()
    out_ref[...] = jnp.zeros_like(out_ref)
    for copy in copies:
        copy.wait()
    out_ref[:, :krylov] = coef_ref[...]
    row = lax.broadcasted_iota(jnp.int32, (cols, cols), 0)
    lane = lax.broadcasted_iota(jnp.int32, (cols, cols), 1)
    values = jnp.broadcast_to(value_ref[...].astype(jnp.float32), (cols, cols))
    column = jnp.sum(jnp.where(row == lane, values, 0.0), axis=1, keepdims=True)
    out_ref[:, SHIFT_AT:] = jnp.broadcast_to(column, (cols, LANES)).astype(jnp.bfloat16)


def stage_kernel(basis_ref, image_ref, basis_out, image_out, landing, arrived, *, per_step):
    outer = basis_ref.shape[1]
    steps = outer // per_step
    copies = []
    for which, ref in enumerate((basis_ref, image_ref)):
        for j in range(steps):
            at = which * steps + j
            copy = pltpu.make_async_copy(
                ref.at[:, pl.ds(j * per_step, per_step), :], landing.at[at], arrived.at[at]
            )
            copy.start()
            copies.append(copy)
    for which, out in enumerate((basis_out, image_out)):
        for j in range(steps):
            at = which * steps + j
            copies[at].wait()
            out[pl.ds(j * per_step, per_step)] = jnp.swapaxes(landing[at], 0, 1)


def power_of_two(exponent, sign):
    out = jnp.ones(exponent.shape, jnp.float32)
    whole = exponent.astype(jnp.int32)
    for bit in range(7):
        out = out * jnp.where((whole & (1 << bit)) != 0, 2.0 ** (sign * (1 << bit)), 1.0)
    return out


def project_kernel(*refs, groups):
    coef_refs, (basis_ref, image_ref) = refs[:groups], refs[groups : groups + 2]
    own_ref = refs[groups + 2]
    chunk_refs = refs[groups + 3 : 2 * groups + 2]
    sum_ref, held = refs[2 * groups + 2 :]
    outer, krylov, _ = basis_ref.shape
    cols = coef_refs[0].shape[0]
    wanted = groups * cols
    coefs = jnp.concatenate([ref[:, :krylov].astype(jnp.float32) for ref in coef_refs])
    coefs = coefs.astype(jnp.bfloat16)
    shift = jnp.concatenate([ref[:, SHIFT_AT:].astype(jnp.float32) for ref in coef_refs])
    shift = jnp.concatenate([shift, shift], axis=1)
    zeros = jnp.zeros((wanted, 2 * LANES), jnp.float32)
    squares, peaks = [zeros, zeros], [zeros, zeros]
    for pair in range(0, outer, 2):
        fields = []
        for ref in (basis_ref, image_ref):
            both = jnp.concatenate([ref[pair], ref[pair + 1]], axis=1)
            fields.append(jnp.dot(coefs, both, preferred_element_type=jnp.float32))
        ritz, resid = fields[0], fields[1] - shift * fields[0]
        for which, value in enumerate((ritz, resid)):
            squares[which] += value * value
            peaks[which] = jnp.maximum(peaks[which], jnp.abs(value))
            for half in range(2):
                held[pair + half, pl.ds(which * wanted, wanted)] = value[:, half * LANES : (half + 1) * LANES]
    sums = [jnp.sum(x, axis=1, keepdims=True) for x in squares]
    row = lax.broadcasted_iota(jnp.int32, (wanted, LANES), 0)
    lane = lax.broadcasted_iota(jnp.int32, (wanted, LANES), 1)
    line = jnp.where(lane == row, sums[0], 0.0) + jnp.where(lane == row + wanted, sums[1], 0.0)
    sum_ref[...] = jnp.broadcast_to(jnp.sum(line, axis=0, keepdims=True), sum_ref.shape)
    for which in range(2):
        peak = jnp.max(peaks[which], axis=1, keepdims=True)
        exponent = jnp.clip(jnp.floor(14.0 - jnp.log(peak) * 1.4426950408889634), 0.0, 100.0)
        exponent = jnp.broadcast_to(exponent, (wanted, LANES))
        scale = power_of_two(exponent, 1)
        for s in range(groups):
            at = s * cols
            block = jnp.swapaxes(held[:, pl.ds(which * wanted + at, cols), :], 0, 1)
            if s == 0:
                own_ref[which * cols : (which + 1) * cols] = block
            else:
                block = block * scale[at : at + cols][:, None, :]
                ref = chunk_refs[s - 1]
                ref[pl.ds(which * cols * outer, cols * outer), :] = block.reshape(cols * outer, LANES)
                ref[pl.ds(2 * cols * outer + which * cols, cols), :] = exponent[at : at + cols]


def finish_kernel(*refs, groups, rows_total):
    own_ref, chunk_refs, line_refs = refs[0], refs[1:groups], refs[groups : 2 * groups]
    outs, norm_ref = refs[2 * groups : 2 * groups + 2], refs[2 * groups + 2]
    double, outer, _ = own_ref.shape
    cols = double // 2
    row = lax.broadcasted_iota(jnp.int32, (cols, LANES), 0)
    lane = lax.broadcasted_iota(jnp.int32, (cols, LANES), 1)
    ritz, resid = jnp.zeros((cols, LANES), jnp.float32), jnp.zeros((cols, LANES), jnp.float32)
    for s, ref in enumerate(line_refs):
        ritz += jnp.where(lane == row + s * cols, ref[...], 0.0)
        resid += jnp.where(lane == row + (s + groups) * cols, ref[...], 0.0)
    ritz = jnp.sum(ritz, axis=1, keepdims=True) + 1.0
    resid = jnp.sum(resid, axis=1, keepdims=True)
    factor = jnp.broadcast_to(jnp.sqrt(rows_total / ritz), (cols, LANES))
    norms = jnp.sqrt(resid / ritz)
    norm_ref[...] = jnp.sum(jnp.where(lane == row, norms, 0.0), axis=0, keepdims=True)[:, :cols]
    me = lax.axis_index("grp")
    for s in range(groups):
        source = lax.rem(me + groups - s, groups)
        at = pl.ds(pl.multiple_of(source * LANES, LANES), LANES)
        for which in range(2):
            if s == 0:
                block = own_ref[which * cols : (which + 1) * cols]
                gain = factor
            else:
                ref = chunk_refs[s - 1]
                block = ref[pl.ds(which * cols * outer, cols * outer), :].reshape(cols, outer, LANES)
                exponent = ref[pl.ds(2 * cols * outer + which * cols, cols), :]
                gain = factor * power_of_two(exponent, -1)
            outs[which][:, :, at] = block * gain[:, None, :]


def shifted(value, s, groups):
    return lax.ppermute(value, "grp", [(i, (i + s) % groups) for i in range(groups)])


def in_hbm(value):
    return pltpu.with_memory_space_constraint(value, pltpu.HBM)


def grant(mib):
    return pltpu.CompilerParams(vmem_limit_bytes=mib << 20)


def body(krylov_basis, krylov_image, tridiag_vectors, ritz_values):
    groups = lax.axis_size("grp")
    members = lax.axis_size("row")
    krylov, outer, inner = krylov_basis.shape
    cols = tridiag_vectors.shape[1]
    wanted = groups * cols
    rows_total = float(outer * inner * groups * members)
    f32 = jnp.float32
    own_coefs = pl.pallas_call(
        pack_kernel,
        out_shape=jax.ShapeDtypeStruct((cols, SHIFT_AT + LANES), jnp.bfloat16),
        in_specs=[pl.BlockSpec(memory_space=pltpu.HBM)] * 2,
        scratch_shapes=[
            pltpu.VMEM((cols, krylov), jnp.bfloat16),
            pltpu.VMEM((1, cols), jnp.bfloat16),
            pltpu.SemaphoreType.DMA((2,)),
        ],
        compiler_params=grant(1),
        name="pack",
    )(in_hbm(tridiag_vectors.T), in_hbm(ritz_values[None, :]))
    coefs = [own_coefs] + [shifted(own_coefs, groups - s, groups) for s in range(1, groups)]

    per_step = 16
    basis, image, _ = lax.optimization_barrier((krylov_basis, krylov_image, own_coefs))
    turned = jax.ShapeDtypeStruct((outer, krylov, inner), krylov_basis.dtype)
    basis, image = pl.pallas_call(
        functools.partial(stage_kernel, per_step=per_step),
        in_specs=[pl.BlockSpec(memory_space=pltpu.HBM)] * 2,
        out_shape=[turned] * 2,
        scratch_shapes=[
            pltpu.VMEM((2 * outer // per_step, krylov, per_step, inner), krylov_basis.dtype),
            pltpu.SemaphoreType.DMA((2 * outer // per_step,)),
        ],
        cost_estimate=pl.CostEstimate(flops=3 << 30, bytes_accessed=2 * krylov_basis.size * 2, transcendentals=0),
        compiler_params=grant(26),
        name="stage",
    )(in_hbm(basis), in_hbm(image))

    chunk = (2 * cols * (outer + 1), LANES)
    shapes = [(2 * cols, outer, LANES)] + [chunk] * (groups - 1) + [(members, LANES)]
    outs = pl.pallas_call(
        functools.partial(project_kernel, groups=groups),
        out_shape=[jax.ShapeDtypeStruct(shape, f32) for shape in shapes],
        scratch_shapes=[pltpu.VMEM((outer, 2 * wanted, LANES), f32)],
        compiler_params=grant(20),
        name="project",
    )(*coefs, basis, image)
    own, chunks, sums = outs[0], outs[1:groups], outs[groups]
    totals = lax.all_to_all(sums[:, None, :], "row", split_axis=0, concat_axis=0, tiled=True)
    sent = [shifted(c.astype(jnp.float16), s + 1, groups) for s, c in enumerate(chunks)]
    chunks = [c.astype(f32) for c in sent]
    total = totals.sum(axis=0)
    lines = [total] + [shifted(total, s, groups) for s in range(1, groups)]
    ritz, resid, norms = pl.pallas_call(
        functools.partial(finish_kernel, groups=groups, rows_total=rows_total),
        out_shape=[jax.ShapeDtypeStruct((cols, outer, groups * inner), f32)] * 2
        + [jax.ShapeDtypeStruct((1, cols), f32)],
        compiler_params=grant(12),
        name="finish",
    )(own, *chunks, *lines)
    return ritz, resid, norms.reshape(cols)


def solution(mesh):
    placed = (P(None, "row", "grp"), P(None, "row", "grp"), P(None, "grp"), P("grp"))
    return jax.shard_map(
        body,
        mesh=mesh,
        in_specs=placed,
        out_specs=(P("grp", "row", None), P("grp", "row", None), P("grp")),
        check_vma=False,
    )
```

time: 59.4 us -> 49.2 us (0.83)
  blocking collectives: 0 us -> 22.8 us
  starting transfers between devices: 27.7 us -> 12.2 us
  other arithmetic: 6.44 us -> 0.31 us
  waiting for transfers between devices: 8.55 us -> 2.73 us
  local copies, waits for them, and re-layouts: 3.01 us -> 0 us
  Pallas kernels: 12.6 us -> 10.2 us
    all_to_all x0 -> x1, blocking collectives: none -> 22.8 us  [body(): lax.all_to_all(sums[:, None, :], 'row', split_axis=0, concat_axis=0, tile...]
    all_to_all x1 -> x0, starting transfers between devices: 15.4 us -> none  [everyone(): return lax.all_to_all(copies, axis, split_axis=0, concat_axis=0, tiled=True)]
    all_to_all x1 -> x0, waiting for transfers between devices: 6.69 us -> none  [everyone(): return lax.all_to_all(copies, axis, split_axis=0, concat_axis=0, tiled=True)]
    convert_element_type x3, other arithmetic: 3.25 us -> 0.11 us  [body(): c.astype(jnp.float16)]
    convert_element_type x3, other arithmetic: 2.53 us -> 0.11 us  [body(): chunks = [c.astype(f32) for c in sent]]
    pallas_call x1, Pallas kernels: 3.09 us -> 1.56 us  [body(): pl.pallas_call(functools.partial(finish_kernel, groups=groups, rows_total...]
    unnamed x8 -> x0, local copies, waits for them, and re-layouts: 1.2 us -> none
    squeeze x1 -> x0, local copies, waits for them, and re-layouts: 1.18 us -> none  [body(): return (ritz, resid, norms[0, :cols])]
  transfers between devices with their start and end apart: 10 -> 9, of which waited for: 3 -> 2; matrix products, arithmetic and copies ran while one was open for 12% -> 1% of each run, Pallas kernels for 0% -> 12%
where the time goes in v2:
time: 49.2 us; the launch traced here: 49 us
  blocking collectives  22.8 us (46%)
  starting transfers between devices  12.2 us (25%)
  Pallas kernels  10.2 us (21%)
  waiting for transfers between devices  2.73 us (6%)
  between operations  0.76 us (2%)
    all_to_all x1, blocking collectives, body(): lax.all_to_all(sums[:, None, :], 'row', split_axis=0, concat_axis=0, tile...  22.8 us
    ppermute x9, starting transfers between devices, shifted(): lax.ppermute(value, 'grp', [(i, (i + s) % groups) for i in range(groups)])  12.2 us
    pallas_call x1, Pallas kernels, body(): pl.pallas_call(functools.partial(stage_kernel, per_step=per_step), in_spe...  5.73 us
    ppermute x9, waiting for transfers between devices, shifted(): lax.ppermute(value, 'grp', [(i, (i + s) % groups) for i in range(groups)])  2.73 us
    pallas_call x1, Pallas kernels, body(): pl.pallas_call(functools.partial(project_kernel, groups=groups), out_shap...  2.16 us
    pallas_call x1, Pallas kernels, body(): pl.pallas_call(functools.partial(finish_kernel, groups=groups, rows_total...  1.56 us
  transfers between devices with their start and end apart: 9, of which 2 were waited for; matrix products, arithmetic and copies ran while one was open for 1% of the time, Pallas kernels for 12%

profile of v2, /device:TPU:1, one launch (start us, length us, event | category | flops | bytes accessed | tf_op | source)
XLA Modules:
  0.0 49.0 jit_solution(13195455983969499523)
XLA Ops:
  0.6 0.8 %pack.1.refs_0_ = bf16[8,512]{1,0:T(8,128)(2,1)S(1)} custom-call(bf16[8,300]{1,0:T(8,128)(2,1)} %bitcast.12, bf16[1,8]{1,0:T(2,128)(2,1)} %bitcast.13), custom_call_target="tpu_custom_call" | custom-call | tf_op jit(solution)/shard_map/pack/pallas_call | solution.py:160
  1.4 2.1 %collective-permute-start.2 = (bf16[8,512]{1,0:T(8,128)(2,1)S(1)}, bf16[8,512]{1,0:T(8,128)(2,1)S(1)}, u32[]{:S(2)}, u32[]{:S(2)}) collective-permute-start(bf16[8,512]{1,0:T(8,128)(2,1)S(1)} %pack.1.refs_0_), channel_id=1, source_target_pairs={{0,64},{64,128},{128,192},{192,0},{1,65},{65,129},{129,193},{193,1... | collective-permute-start | bytes 24584 | tf_op jit(solution)/shard_map/ppermute | solution.py:141
  3.5 2.5 %collective-permute-start.1 = (bf16[8,512]{1,0:T(8,128)(2,1)S(1)}, bf16[8,512]{1,0:T(8,128)(2,1)S(1)}, u32[]{:S(2)}, u32[]{:S(2)}) collective-permute-start(bf16[8,512]{1,0:T(8,128)(2,1)S(1)} %pack.1.refs_0_), channel_id=1, source_target_pairs={{0,128},{64,192},{128,0},{192,64},{1,129},{65,193},{129,1},{193,65... | collective-permute-start | bytes 24584 | tf_op jit(solution)/shard_map/ppermute | solution.py:141
  6.0 1.2 %collective-permute-start = (bf16[8,512]{1,0:T(8,128)(2,1)S(1)}, bf16[8,512]{1,0:T(8,128)(2,1)S(1)}, u32[]{:S(2)}, u32[]{:S(2)}) collective-permute-start(bf16[8,512]{1,0:T(8,128)(2,1)S(1)} %pack.1.refs_0_), channel_id=1, source_target_pairs={{0,192},{64,0},{128,64},{192,128},{1,193},{65,1},{129,65},{193,129... | collective-permute-start | bytes 24584 | tf_op jit(solution)/shard_map/ppermute | solution.py:141
  7.1 5.7 %stage.1 = (bf16[64,300,128]{2,1,0:T(8,128)(2,1)S(1)}, bf16[64,300,128]{2,1,0:T(8,128)(2,1)S(1)}) custom-call(bf16[300,64,128]{2,1,0:T(8,128)(2,1)} %basis_ref, bf16[300,64,128]{2,1,0:T(8,128)(2,1)} %image_ref), custom_call_target="tpu_custom_call" | custom-call | flops 3221225472 | bytes 9830400 | tf_op jit(solution)/shard_map/stage/pallas_call | solution.py:177
  12.9 0.0 collective-permute-done.2.refs_3_
  12.9 0.0 collective-permute-done.1.refs_2_
  12.9 0.0 collective-permute-done.refs_1_
  12.9 2.2 %project.1 = (f32[16,64,128]{2,1,0:T(8,128)S(1)}, f32[1040,128]{1,0:T(8,128)S(1)}, f32[1040,128]{1,0:T(8,128)S(1)}, f32[1040,128]{1,0:T(8,128)S(1)}, f32[64,128]{1,0:T(8,128)S(1)}) custom-call(bf16[8,512]{1,0:T(8,128)(2,1)S(1)} %pack.1.refs_0_, bf16[8,512]{1,0:T(8,128)(2,1)S(1)} %collective-permute-done.refs_1_, ...), custom_call_target="tpu_custom_call" | custom-call | tf_op jit(solution)/shard_map/project/pallas_call | solution.py:192
  15.1 0.1 collective-permute-start.5
  15.3 2.2 %collective-permute-start.4 = (f16[1040,128]{1,0:T(8,128)(2,1)S(1)}, f16[1040,128]{1,0:T(8,128)(2,1)S(1)}, u32[]{:S(2)}, u32[]{:S(2)}) collective-permute-start(f16[1040,128]{1,0:T(8,128)(2,1)S(1)} %convert_element_type.20), channel_id=1, source_target_pairs={{0,128},{64,192},{128,0},{192,64},{1,129},{65,193},{129,1},{193,65... | collective-permute-start | bytes 798728 | tf_op jit(solution)/shard_map/ppermute | solution.py:141
  17.5 0.1 collective-permute-start.3
  17.6 22.8 %all_to_all.5 = f32[64,1,128]{2,1,0:T(1,128)S(1)} all-to-all(f32[64,1,128]{2,1,0:T(1,128)S(1)} %bitcast.7), channel_id=1, replica_groups=mesh['grp'=4,'row'=64] {'row'}, dimensions={0} | all-to-all | bytes 65536 | tf_op jit(solution)/shard_map/all_to_all | solution.py:200
  40.4 0.1 reduce_sum.11
  40.5 3.0 %collective-permute-start.8 = (f32[1,128]{1,0:T(1,128)S(1)}, f32[1,128]{1,0:T(1,128)S(1)}, u32[]{:S(2)}, u32[]{:S(2)}) collective-permute-start(f32[1,128]{1,0:T(1,128)S(1)} %bitcast.8), channel_id=1, source_target_pairs={{0,192},{64,0},{128,64},{192,128},{1,193},{65,1},{129,65},{193,129... | collective-permute-start | bytes 1544 | tf_op jit(solution)/shard_map/ppermute | solution.py:141
  43.5 0.4 collective-permute-start.7
  43.9 0.0 collective-permute-done.5
  43.9 0.8 %collective-permute-start.6 = (f32[1,128]{1,0:T(1,128)S(1)}, f32[1,128]{1,0:T(1,128)S(1)}, u32[]{:S(2)}, u32[]{:S(2)}) collective-permute-start(f32[1,128]{1,0:T(1,128)S(1)} %bitcast.10), channel_id=1, source_target_pairs={{0,64},{64,128},{128,192},{192,0},{1,65},{65,129},{129,193},{193,1... | collective-permute-start | bytes 1544 | tf_op jit(solution)/shard_map/ppermute | solution.py:141
  44.7 0.0 collective-permute-done.4
  44.7 0.0 collective-permute-done.3
  44.8 0.0 collective-permute-done.8.refs_7_
  44.8 2.6 %collective-permute-done.7.refs_6_ = f32[1,128]{1,0:T(1,128)S(1)} collective-permute-done((f32[1,128]{1,0:T(1,128)S(1)}, f32[1,128]{1,0:T(1,128)S(1)}, u32[]{:S(2)}, u32[]{:S(2)}) %collective-permute-start.7) | collective-permute-done | bytes 544 | tf_op jit(solution)/shard_map/ppermute | solution.py:141
  47.4 0.1 collective-permute-done.6.refs_5_
  47.5 1.6 %finish.1 = (f32[8,64,512]{2,1,0:T(8,128)}, f32[8,64,512]{2,1,0:T(8,128)}, f32[1,8]{1,0:T(1,128)}) custom-call(f32[16,64,128]{2,1,0:T(8,128)S(1)} %get-tuple-element.19.refs_0_, f32[1040,128]{1,0:T(8,128)S(1)} %convert_element_type.19.refs_1_, f32[1040,128]{1,0:T(8,128)S(1)} %convert_element_type.21.refs_2_, f32[1040,128]{1,0:T(8,128)S(1)} %convert_element_type.23.refs_3_, ...), custom_call_target="tpu_custom_call" | custom-call | tf_op jit(solution)/shard_map/finish/pallas_call | solution.py:205
  (6 shorter events, 0.2 us)
Async XLA Ops:
  1.4 11.5 %collective-permute-start.2 = (bf16[8,512]{1,0:T(8,128)(2,1)S(1)}, bf16[8,512]{1,0:T(8,128)(2,1)S(1)}, u32[]{:S(2)}, u32[]{:S(2)}) collective-permute-start(bf16[8,512]{1,0:T(8,128)(2,1)S(1)} %pack.1.refs_0_), channel_id=1, source_target_pairs={{0,64},{64,128},{128,192},{192,0},{1,65},{65,129},{129,193},{193,1... | collective-permute-start | bytes 24584 | tf_op jit(solution)/shard_map/ppermute | solution.py:141
  3.5 9.4 %collective-permute-start.1 = (bf16[8,512]{1,0:T(8,128)(2,1)S(1)}, bf16[8,512]{1,0:T(8,128)(2,1)S(1)}, u32[]{:S(2)}, u32[]{:S(2)}) collective-permute-start(bf16[8,512]{1,0:T(8,128)(2,1)S(1)} %pack.1.refs_0_), channel_id=1, source_target_pairs={{0,128},{64,192},{128,0},{192,64},{1,129},{65,193},{129,1},{193,65... | collective-permute-start | bytes 24584 | tf_op jit(solution)/shard_map/ppermute | solution.py:141
  6.0 6.9 %collective-permute-start = (bf16[8,512]{1,0:T(8,128)(2,1)S(1)}, bf16[8,512]{1,0:T(8,128)(2,1)S(1)}, u32[]{:S(2)}, u32[]{:S(2)}) collective-permute-start(bf16[8,512]{1,0:T(8,128)(2,1)S(1)} %pack.1.refs_0_), channel_id=1, source_target_pairs={{0,192},{64,0},{128,64},{192,128},{1,193},{65,1},{129,65},{193,129... | collective-permute-start | bytes 24584 | tf_op jit(solution)/shard_map/ppermute | solution.py:141
  15.1 28.7 %collective-permute-start.5 = (f16[1040,128]{1,0:T(8,128)(2,1)S(1)}, f16[1040,128]{1,0:T(8,128)(2,1)S(1)}, u32[]{:S(2)}, u32[]{:S(2)}) collective-permute-start(f16[1040,128]{1,0:T(8,128)(2,1)S(1)} %convert_element_type.22), channel_id=1, source_target_pairs={{0,192},{64,0},{128,64},{192,128},{1,193},{65,1},{129,65},{193,129... | collective-permute-start | bytes 798728 | tf_op jit(solution)/shard_map/ppermute | solution.py:141
  15.3 29.4 %collective-permute-start.4 = (f16[1040,128]{1,0:T(8,128)(2,1)S(1)}, f16[1040,128]{1,0:T(8,128)(2,1)S(1)}, u32[]{:S(2)}, u32[]{:S(2)}) collective-permute-start(f16[1040,128]{1,0:T(8,128)(2,1)S(1)} %convert_element_type.20), channel_id=1, source_target_pairs={{0,128},{64,192},{128,0},{192,64},{1,129},{65,193},{129,1},{193,65... | collective-permute-start | bytes 798728 | tf_op jit(solution)/shard_map/ppermute | solution.py:141
  17.5 27.2 %collective-permute-start.3 = (f16[1040,128]{1,0:T(8,128)(2,1)S(1)}, f16[1040,128]{1,0:T(8,128)(2,1)S(1)}, u32[]{:S(2)}, u32[]{:S(2)}) collective-permute-start(f16[1040,128]{1,0:T(8,128)(2,1)S(1)} %convert_element_type.18), channel_id=1, source_target_pairs={{0,64},{64,128},{128,192},{192,0},{1,65},{65,129},{129,193},{193,1... | collective-permute-start | bytes 798728 | tf_op jit(solution)/shard_map/ppermute | solution.py:141
  40.5 4.3 %collective-permute-start.8 = (f32[1,128]{1,0:T(1,128)S(1)}, f32[1,128]{1,0:T(1,128)S(1)}, u32[]{:S(2)}, u32[]{:S(2)}) collective-permute-start(f32[1,128]{1,0:T(1,128)S(1)} %bitcast.8), channel_id=1, source_target_pairs={{0,192},{64,0},{128,64},{192,128},{1,193},{65,1},{129,65},{193,129... | collective-permute-start | bytes 1544 | tf_op jit(solution)/shard_map/ppermute | solution.py:141
  43.5 3.9 %collective-permute-start.7 = (f32[1,128]{1,0:T(1,128)S(1)}, f32[1,128]{1,0:T(1,128)S(1)}, u32[]{:S(2)}, u32[]{:S(2)}) collective-permute-start(f32[1,128]{1,0:T(1,128)S(1)} %bitcast.9), channel_id=1, source_target_pairs={{0,128},{64,192},{128,0},{192,64},{1,129},{65,193},{129,1},{193,65... | collective-permute-start | bytes 1544 | tf_op jit(solution)/shard_map/ppermute | solution.py:141
  43.9 3.6 %collective-permute-start.6 = (f32[1,128]{1,0:T(1,128)S(1)}, f32[1,128]{1,0:T(1,128)S(1)}, u32[]{:S(2)}, u32[]{:S(2)}) collective-permute-start(f32[1,128]{1,0:T(1,128)S(1)} %bitcast.10), channel_id=1, source_target_pairs={{0,64},{64,128},{128,192},{192,0},{1,65},{65,129},{129,193},{193,1... | collective-permute-start | bytes 1544 | tf_op jit(solution)/shard_map/ppermute | solution.py:141

commit v3 on v2

--- a/solution.py
+++ b/solution.py
@@ -10,6 +10,7 @@
 
 LANES = 128
 SHIFT_AT = 384
+LEADER = 41
 
 
 def pack_kernel(coef_hbm, value_hbm, out_ref, coef_ref, value_ref, arrived):
@@ -31,23 +32,14 @@
     out_ref[:, SHIFT_AT:] = jnp.broadcast_to(column, (cols, LANES)).astype(jnp.bfloat16)
 
 
-def stage_kernel(basis_ref, image_ref, basis_out, image_out, landing, arrived, *, per_step):
-    outer = basis_ref.shape[1]
-    steps = outer // per_step
-    copies = []
-    for which, ref in enumerate((basis_ref, image_ref)):
-        for j in range(steps):
-            at = which * steps + j
-            copy = pltpu.make_async_copy(
-                ref.at[:, pl.ds(j * per_step, per_step), :], landing.at[at], arrived.at[at]
-            )
-            copy.start()
-            copies.append(copy)
-    for which, out in enumerate((basis_out, image_out)):
-        for j in range(steps):
-            at = which * steps + j
-            copies[at].wait()
-            out[pl.ds(j * per_step, per_step)] = jnp.swapaxes(landing[at], 0, 1)
+def stage_kernel(basis_ref, image_ref, basis_out, image_out):
+    krylov, outer, _ = basis_ref.shape
+    for ref, out in ((basis_ref, basis_out), (image_ref, image_out)):
+        for j in range(0, outer, 8):
+            for k in range(0, krylov, 16):
+                some = min(16, krylov - k)
+                block = ref[pl.ds(k, some), pl.ds(j, 8), :]
+                out[pl.ds(j, 8), pl.ds(k, some), :] = jnp.swapaxes(block, 0, 1)
 
 
 def power_of_two(exponent, sign):
@@ -106,8 +98,8 @@
 
 
 def finish_kernel(*refs, groups, rows_total):
-    own_ref, chunk_refs, line_refs = refs[0], refs[1:groups], refs[groups : 2 * groups]
-    outs, norm_ref = refs[2 * groups : 2 * groups + 2], refs[2 * groups + 2]
+    own_ref, chunk_refs, line_refs = refs[0], refs[1:groups], refs[groups:-3]
+    outs, norm_ref = refs[-3:-1], refs[-1]
     double, outer, _ = own_ref.shape
     cols = double // 2
     row = lax.broadcasted_iota(jnp.int32, (cols, LANES), 0)
@@ -166,26 +158,21 @@
             pltpu.VMEM((1, cols), jnp.bfloat16),
             pltpu.SemaphoreType.DMA((2,)),
         ],
+        cost_estimate=pl.CostEstimate(flops=6 << 30, bytes_accessed=16 << 20, transcendentals=0),
         compiler_params=grant(1),
         name="pack",
     )(in_hbm(tridiag_vectors.T), in_hbm(ritz_values[None, :]))
     coefs = [own_coefs] + [shifted(own_coefs, groups - s, groups) for s in range(1, groups)]
 
-    per_step = 16
-    basis, image, _ = lax.optimization_barrier((krylov_basis, krylov_image, own_coefs))
+    basis, image = krylov_basis, krylov_image
     turned = jax.ShapeDtypeStruct((outer, krylov, inner), krylov_basis.dtype)
     basis, image = pl.pallas_call(
-        functools.partial(stage_kernel, per_step=per_step),
-        in_specs=[pl.BlockSpec(memory_space=pltpu.HBM)] * 2,
+        stage_kernel,
         out_shape=[turned] * 2,
-        scratch_shapes=[
-            pltpu.VMEM((2 * outer // per_step, krylov, per_step, inner), krylov_basis.dtype),
-            pltpu.SemaphoreType.DMA((2 * outer // per_step,)),
-        ],
         cost_estimate=pl.CostEstimate(flops=3 << 30, bytes_accessed=2 * krylov_basis.size * 2, transcendentals=0),
-        compiler_params=grant(26),
+        compiler_params=grant(4),
         name="stage",
-    )(in_hbm(basis), in_hbm(image))
+    )(basis, image)
 
     chunk = (2 * cols * (outer + 1), LANES)
     shapes = [(2 * cols, outer, LANES)] + [chunk] * (groups - 1) + [(members, LANES)]
@@ -197,11 +184,17 @@
         name="project",
     )(*coefs, basis, image)
     own, chunks, sums = outs[0], outs[1:groups], outs[groups]
-    totals = lax.all_to_all(sums[:, None, :], "row", split_axis=0, concat_axis=0, tiled=True)
     sent = [shifted(c.astype(jnp.float16), s + 1, groups) for s, c in enumerate(chunks)]
     chunks = [c.astype(f32) for c in sent]
-    total = totals.sum(axis=0)
-    lines = [total] + [shifted(total, s, groups) for s in range(1, groups)]
+    line = sums[:1]
+    moved = [line] + [shifted(line, s, groups) for s in range(1, groups)]
+    wide = lax.broadcasted_iota(jnp.int32, (1, LANES), 1)
+    total = jnp.zeros((1, LANES), f32)
+    for s, m in enumerate(moved):
+        here = (wide // cols) % groups == s
+        total = total + jnp.roll(jnp.where(here, m, 0.0), -s * cols, axis=1)
+    totals = lax.all_to_all(jnp.broadcast_to(total[None], (members, 1, LANES)), "row", split_axis=0, concat_axis=0, tiled=True, axis_index_groups=[[(r + LEADER) % members for r in range(members)]])
+    lines = [totals.sum(axis=0)]
     ritz, resid, norms = pl.pallas_call(
         functools.partial(finish_kernel, groups=groups, rows_total=rows_total),
         out_shape=[jax.ShapeDtypeStruct((cols, outer, groups * inner), f32)] * 2

time: 49.2 us -> 39.2 us (0.80)
  blocking collectives: 22.8 us -> 18.9 us
  waiting for transfers between devices: 2.73 us -> 0.02 us
  Pallas kernels: 10.2 us -> 7.64 us
  starting transfers between devices: 12.2 us -> 11.2 us
    all_to_all x1, blocking collectives: 22.8 us -> 18.9 us  [body(): lax.all_to_all(jnp.broadcast_to(total[None], (members, 1, LANES)), 'row',...]
    pallas_call x1, Pallas kernels: 5.73 us -> 2.95 us  [body(): pl.pallas_call(stage_kernel, out_shape=[turned] * 2, cost_estimate=pl.Cos...]
    ppermute x9, waiting for transfers between devices: 2.73 us -> 0.02 us  [shifted(): lax.ppermute(value, 'grp', [(i, (i + s) % groups) for i in range(groups)])]
    ppermute x9, starting transfers between devices: 12.2 us -> 11.2 us  [shifted(): lax.ppermute(value, 'grp', [(i, (i + s) % groups) for i in range(groups)])]
  transfers between devices with their start and end apart: 9 -> 9, of which waited for: 2 -> 0; matrix products, arithmetic and copies ran while one was open for 1% -> 1% of each run, Pallas kernels for 12% -> 8%
where the time goes in v3:
time: 39.2 us; the launch traced here: 39.1 us
  blocking collectives  18.9 us (48%)
  starting transfers between devices  11.2 us (29%)
  Pallas kernels  7.64 us (19%)
  between operations  0.78 us (2%)
    all_to_all x1, blocking collectives, body(): lax.all_to_all(jnp.broadcast_to(total[None], (members, 1, LANES)), 'row',...  18.9 us
    ppermute x9, starting transfers between devices, shifted(): lax.ppermute(value, 'grp', [(i, (i + s) % groups) for i in range(groups)])  11.2 us
    pallas_call x1, Pallas kernels, body(): pl.pallas_call(stage_kernel, out_shape=[turned] * 2, cost_estimate=pl.Cos...  2.95 us
    pallas_call x1, Pallas kernels, body(): pl.pallas_call(functools.partial(project_kernel, groups=groups), out_shap...  2.2 us
    pallas_call x1, Pallas kernels, body(): pl.pallas_call(functools.partial(finish_kernel, groups=groups, rows_total...  1.56 us
    pallas_call x1, Pallas kernels, body(): pl.pallas_call(pack_kernel, out_shape=jax.ShapeDtypeStruct((cols, SHIFT_A...  0.94 us
  transfers between devices with their start and end apart: 9, of which 0 were waited for; matrix products, arithmetic and copies ran while one was open for 1% of the time, Pallas kernels for 8%

profile of v3, /device:TPU:1, one launch (start us, length us, event | category | flops | bytes accessed | tf_op | source)
XLA Modules:
  0.0 39.1 jit_solution(3382877040216687498)
XLA Ops:
  0.7 0.9 %pack.1.refs_0_ = bf16[8,512]{1,0:T(8,128)(2,1)S(1)} custom-call(bf16[8,300]{1,0:T(8,128)(2,1)} %bitcast.15, bf16[1,8]{1,0:T(2,128)(2,1)} %bitcast.16), custom_call_target="tpu_custom_call" | custom-call | flops 6442450944 | bytes 16777216 | tf_op jit(solution)/shard_map/pack/pallas_call | solution.py:152
  1.6 2.1 %collective-permute-start.2 = (bf16[8,512]{1,0:T(8,128)(2,1)S(1)}, bf16[8,512]{1,0:T(8,128)(2,1)S(1)}, u32[]{:S(2)}, u32[]{:S(2)}) collective-permute-start(bf16[8,512]{1,0:T(8,128)(2,1)S(1)} %pack.1.refs_0_), channel_id=1, source_target_pairs={{0,64},{64,128},{128,192},{192,0},{1,65},{65,129},{129,193},{193,1... | collective-permute-start | bytes 24584 | tf_op jit(solution)/shard_map/ppermute | solution.py:133
  3.7 2.5 %collective-permute-start.1 = (bf16[8,512]{1,0:T(8,128)(2,1)S(1)}, bf16[8,512]{1,0:T(8,128)(2,1)S(1)}, u32[]{:S(2)}, u32[]{:S(2)}) collective-permute-start(bf16[8,512]{1,0:T(8,128)(2,1)S(1)} %pack.1.refs_0_), channel_id=1, source_target_pairs={{0,128},{64,192},{128,0},{192,64},{1,129},{65,193},{129,1},{193,65... | collective-permute-start | bytes 24584 | tf_op jit(solution)/shard_map/ppermute | solution.py:133
  6.2 1.2 %collective-permute-start = (bf16[8,512]{1,0:T(8,128)(2,1)S(1)}, bf16[8,512]{1,0:T(8,128)(2,1)S(1)}, u32[]{:S(2)}, u32[]{:S(2)}) collective-permute-start(bf16[8,512]{1,0:T(8,128)(2,1)S(1)} %pack.1.refs_0_), channel_id=1, source_target_pairs={{0,192},{64,0},{128,64},{192,128},{1,193},{65,1},{129,65},{193,129... | collective-permute-start | bytes 24584 | tf_op jit(solution)/shard_map/ppermute | solution.py:133
  7.3 2.9 %stage.1 = (bf16[64,300,128]{2,1,0:T(8,128)(2,1)S(1)}, bf16[64,300,128]{2,1,0:T(8,128)(2,1)S(1)}) custom-call(bf16[300,64,128]{2,1,0:T(8,128)(2,1)S(1)} %copy-done, bf16[300,64,128]{2,1,0:T(8,128)(2,1)S(1)} %copy-done.1), custom_call_target="tpu_custom_call" | custom-call | flops 3221225472 | bytes 9830400 | tf_op jit(solution)/shard_map/stage/pallas_call | solution.py:169
  10.3 0.0 collective-permute-done.2.refs_3_
  10.3 0.0 collective-permute-done.refs_1_
  10.3 2.2 %project.1 = (f32[16,64,128]{2,1,0:T(8,128)S(1)}, f32[1040,128]{1,0:T(8,128)S(1)}, f32[1040,128]{1,0:T(8,128)S(1)}, f32[1040,128]{1,0:T(8,128)S(1)}, f32[64,128]{1,0:T(8,128)S(1)}) custom-call(bf16[8,512]{1,0:T(8,128)(2,1)S(1)} %pack.1.refs_0_, bf16[8,512]{1,0:T(8,128)(2,1)S(1)} %collective-permute-done.refs_1_, ...), custom_call_target="tpu_custom_call" | custom-call | tf_op jit(solution)/shard_map/project/pallas_call | solution.py:179
  12.5 0.9 %collective-permute-start.7 = (f32[1,128]{1,0:T(1,128)S(1)}, f32[1,128]{1,0:T(1,128)S(1)}, u32[]{:S(2)}, u32[]{:S(2)}) collective-permute-start(f32[1,128]{1,0:T(1,128)S(1)} %slice.27), channel_id=1, source_target_pairs={{0,128},{64,192},{128,0},{192,64},{1,129},{65,193},{129,1},{193,65... | collective-permute-start | bytes 1544 | tf_op jit(solution)/shard_map/ppermute | solution.py:133
  13.4 0.5 %collective-permute-start.6 = (f32[1,128]{1,0:T(1,128)S(1)}, f32[1,128]{1,0:T(1,128)S(1)}, u32[]{:S(2)}, u32[]{:S(2)}) collective-permute-start(f32[1,128]{1,0:T(1,128)S(1)} %slice.27), channel_id=1, source_target_pairs={{0,64},{64,128},{128,192},{192,0},{1,65},{65,129},{129,193},{193,1... | collective-permute-start | bytes 1544 | tf_op jit(solution)/shard_map/ppermute | solution.py:133
  13.9 2.2 %collective-permute-start.8 = (f32[1,128]{1,0:T(1,128)S(1)}, f32[1,128]{1,0:T(1,128)S(1)}, u32[]{:S(2)}, u32[]{:S(2)}) collective-permute-start(f32[1,128]{1,0:T(1,128)S(1)} %slice.27), channel_id=1, source_target_pairs={{0,192},{64,0},{128,64},{192,128},{1,193},{65,1},{129,65},{193,129... | collective-permute-start | bytes 1544 | tf_op jit(solution)/shard_map/ppermute | solution.py:133
  16.2 0.8 %collective-permute-start.5 = (f16[1040,128]{1,0:T(8,128)(2,1)S(1)}, f16[1040,128]{1,0:T(8,128)(2,1)S(1)}, u32[]{:S(2)}, u32[]{:S(2)}) collective-permute-start(f16[1040,128]{1,0:T(8,128)(2,1)S(1)} %convert_element_type.22), channel_id=1, source_target_pairs={{0,192},{64,0},{128,64},{192,128},{1,193},{65,1},{129,65},{193,129... | collective-permute-start | bytes 798728 | tf_op jit(solution)/shard_map/ppermute | solution.py:133
  17.0 0.4 collective-permute-start.4
  17.4 0.0 collective-permute-done.7
  17.4 0.7 %collective-permute-start.3 = (f16[1040,128]{1,0:T(8,128)(2,1)S(1)}, f16[1040,128]{1,0:T(8,128)(2,1)S(1)}, u32[]{:S(2)}, u32[]{:S(2)}) collective-permute-start(f16[1040,128]{1,0:T(8,128)(2,1)S(1)} %convert_element_type.18), channel_id=1, source_target_pairs={{0,64},{64,128},{128,192},{192,0},{1,65},{65,129},{129,193},{193,1... | collective-permute-start | bytes 798728 | tf_op jit(solution)/shard_map/ppermute | solution.py:133
  18.2 0.1 slice.30
  18.2 0.1 slice.28
  18.3 0.0 collective-permute-done.8
  18.3 0.1 slice.32
  18.4 0.1 fusion.3
  18.5 18.9 %all_to_all.5 = f32[64,1,128]{2,1,0:T(1,128)S(1)} all-to-all(f32[64,1,128]{2,1,0:T(1,128)S(1)} %broadcast_in_dim.21), channel_id=1, replica_groups={{41,42,43,44,45,46,47,48,49,50,51,52,53,54,55,56,57,58,59,60,61,62,63,0..., dimensions={0} | all-to-all | bytes 65536 | tf_op jit(solution)/shard_map/all_to_all | solution.py:196
  37.4 0.0 collective-permute-done.5
  37.4 0.0 collective-permute-done.4
  37.6 1.6 %finish.1 = (f32[8,64,512]{2,1,0:T(8,128)}, f32[8,64,512]{2,1,0:T(8,128)}, f32[1,8]{1,0:T(1,128)}) custom-call(f32[16,64,128]{2,1,0:T(8,128)S(1)} %get-tuple-element.15.refs_0_, f32[1040,128]{1,0:T(8,128)S(1)} %convert_element_type.19.refs_1_, f32[1040,128]{1,0:T(8,128)S(1)} %convert_element_type.21.refs_2_, f32[1040,128]{1,0:T(8,128)S(1)} %convert_element_type.23.refs_3_, ...), custom_call_target="tpu_custom_call" | custom-call | tf_op jit(solution)/shard_map/finish/pallas_call | solution.py:198
  (19 shorter events, 0.3 us)
Async XLA Ops:
  0.6 6.7 %copy-start = (bf16[300,64,128]{2,1,0:T(8,128)(2,1)S(1)}, bf16[300,64,128]{2,1,0:T(8,128)(2,1)}, u32[]{:S(2)}) copy-start(bf16[300,64,128]{2,1,0:T(8,128)(2,1)} %basis_ref.1) | copy-start | bytes 14745604
  0.6 6.7 %copy-start.1 = (bf16[300,64,128]{2,1,0:T(8,128)(2,1)S(1)}, bf16[300,64,128]{2,1,0:T(8,128)(2,1)}, u32[]{:S(2)}) copy-start(bf16[300,64,128]{2,1,0:T(8,128)(2,1)} %image_ref.1) | copy-start | bytes 14745604
  1.6 8.7 %collective-permute-start.2 = (bf16[8,512]{1,0:T(8,128)(2,1)S(1)}, bf16[8,512]{1,0:T(8,128)(2,1)S(1)}, u32[]{:S(2)}, u32[]{:S(2)}) collective-permute-start(bf16[8,512]{1,0:T(8,128)(2,1)S(1)} %pack.1.refs_0_), channel_id=1, source_target_pairs={{0,64},{64,128},{128,192},{192,0},{1,65},{65,129},{129,193},{193,1... | collective-permute-start | bytes 24584 | tf_op jit(solution)/shard_map/ppermute | solution.py:133
  3.7 6.6 %collective-permute-start.1 = (bf16[8,512]{1,0:T(8,128)(2,1)S(1)}, bf16[8,512]{1,0:T(8,128)(2,1)S(1)}, u32[]{:S(2)}, u32[]{:S(2)}) collective-permute-start(bf16[8,512]{1,0:T(8,128)(2,1)S(1)} %pack.1.refs_0_), channel_id=1, source_target_pairs={{0,128},{64,192},{128,0},{192,64},{1,129},{65,193},{129,1},{193,65... | collective-permute-start | bytes 24584 | tf_op jit(solution)/shard_map/ppermute | solution.py:133
  6.2 4.1 %collective-permute-start = (bf16[8,512]{1,0:T(8,128)(2,1)S(1)}, bf16[8,512]{1,0:T(8,128)(2,1)S(1)}, u32[]{:S(2)}, u32[]{:S(2)}) collective-permute-start(bf16[8,512]{1,0:T(8,128)(2,1)S(1)} %pack.1.refs_0_), channel_id=1, source_target_pairs={{0,192},{64,0},{128,64},{192,128},{1,193},{65,1},{129,65},{193,129... | collective-permute-start | bytes 24584 | tf_op jit(solution)/shard_map/ppermute | solution.py:133
  12.5 4.9 %collective-permute-start.7 = (f32[1,128]{1,0:T(1,128)S(1)}, f32[1,128]{1,0:T(1,128)S(1)}, u32[]{:S(2)}, u32[]{:S(2)}) collective-permute-start(f32[1,128]{1,0:T(1,128)S(1)} %slice.27), channel_id=1, source_target_pairs={{0,128},{64,192},{128,0},{192,64},{1,129},{65,193},{129,1},{193,65... | collective-permute-start | bytes 1544 | tf_op jit(solution)/shard_map/ppermute | solution.py:133
  13.4 4.7 %collective-permute-start.6 = (f32[1,128]{1,0:T(1,128)S(1)}, f32[1,128]{1,0:T(1,128)S(1)}, u32[]{:S(2)}, u32[]{:S(2)}) collective-permute-start(f32[1,128]{1,0:T(1,128)S(1)} %slice.27), channel_id=1, source_target_pairs={{0,64},{64,128},{128,192},{192,0},{1,65},{65,129},{129,193},{193,1... | collective-permute-start | bytes 1544 | tf_op jit(solution)/shard_map/ppermute | solution.py:133
  13.9 4.4 %collective-permute-start.8 = (f32[1,128]{1,0:T(1,128)S(1)}, f32[1,128]{1,0:T(1,128)S(1)}, u32[]{:S(2)}, u32[]{:S(2)}) collective-permute-start(f32[1,128]{1,0:T(1,128)S(1)} %slice.27), channel_id=1, source_target_pairs={{0,192},{64,0},{128,64},{192,128},{1,193},{65,1},{129,65},{193,129... | collective-permute-start | bytes 1544 | tf_op jit(solution)/shard_map/ppermute | solution.py:133
  16.2 21.2 %collective-permute-start.5 = (f16[1040,128]{1,0:T(8,128)(2,1)S(1)}, f16[1040,128]{1,0:T(8,128)(2,1)S(1)}, u32[]{:S(2)}, u32[]{:S(2)}) collective-permute-start(f16[1040,128]{1,0:T(8,128)(2,1)S(1)} %convert_element_type.22), channel_id=1, source_target_pairs={{0,192},{64,0},{128,64},{192,128},{1,193},{65,1},{129,65},{193,129... | collective-permute-start | bytes 798728 | tf_op jit(solution)/shard_map/ppermute | solution.py:133
  17.0 20.5 %collective-permute-start.4 = (f16[1040,128]{1,0:T(8,128)(2,1)S(1)}, f16[1040,128]{1,0:T(8,128)(2,1)S(1)}, u32[]{:S(2)}, u32[]{:S(2)}) collective-permute-start(f16[1040,128]{1,0:T(8,128)(2,1)S(1)} %convert_element_type.20), channel_id=1, source_target_pairs={{0,128},{64,192},{128,0},{192,64},{1,129},{65,193},{129,1},{193,65... | collective-permute-start | bytes 798728 | tf_op jit(solution)/shard_map/ppermute | solution.py:133
  17.4 20.1 %collective-permute-start.3 = (f16[1040,128]{1,0:T(8,128)(2,1)S(1)}, f16[1040,128]{1,0:T(8,128)(2,1)S(1)}, u32[]{:S(2)}, u32[]{:S(2)}) collective-permute-start(f16[1040,128]{1,0:T(8,128)(2,1)S(1)} %convert_element_type.18), channel_id=1, source_target_pairs={{0,64},{64,128},{128,192},{192,0},{1,65},{65,129},{129,193},{193,1... | collective-permute-start | bytes 798728 | tf_op jit(solution)/shard_map/ppermute | solution.py:133

commit v4 on v3

--- a/solution.py
+++ b/solution.py
@@ -62,7 +62,7 @@
     coefs = coefs.astype(jnp.bfloat16)
     shift = jnp.concatenate([ref[:, SHIFT_AT:].astype(jnp.float32) for ref in coef_refs])
     shift = jnp.concatenate([shift, shift], axis=1)
-    zeros = jnp.zeros((wanted, 2 * LANES), jnp.float32)
+    zeros = jnp.zeros((wanted, LANES), jnp.float32)
     squares, peaks = [zeros, zeros], [zeros, zeros]
     for pair in range(0, outer, 2):
         fields = []
@@ -71,10 +71,11 @@
             fields.append(jnp.dot(coefs, both, preferred_element_type=jnp.float32))
         ritz, resid = fields[0], fields[1] - shift * fields[0]
         for which, value in enumerate((ritz, resid)):
-            squares[which] += value * value
-            peaks[which] = jnp.maximum(peaks[which], jnp.abs(value))
             for half in range(2):
-                held[pair + half, pl.ds(which * wanted, wanted)] = value[:, half * LANES : (half + 1) * LANES]
+                part = value[:, half * LANES : (half + 1) * LANES]
+                squares[which] += part * part
+                peaks[which] = jnp.maximum(peaks[which], jnp.abs(part))
+                held[pair + half, pl.ds(which * wanted, wanted)] = part
     sums = [jnp.sum(x, axis=1, keepdims=True) for x in squares]
     row = lax.broadcasted_iota(jnp.int32, (wanted, LANES), 0)
     lane = lax.broadcasted_iota(jnp.int32, (wanted, LANES), 1)
@@ -115,7 +116,7 @@
     norm_ref[...] = jnp.sum(jnp.where(lane == row, norms, 0.0), axis=0, keepdims=True)[:, :cols]
     me = lax.axis_index("grp")
     for s in range(groups):
-        source = lax.rem(me + groups - s, groups)
+        source = me ^ s
         at = pl.ds(pl.multiple_of(source * LANES, LANES), LANES)
         for which in range(2):
             if s == 0:
@@ -129,8 +130,19 @@
             outs[which][:, :, at] = block * gain[:, None, :]
 
 
+def total_kernel(*refs, cols):
+    line_refs, out_ref = refs[:-1], refs[-1]
+    groups = len(line_refs)
+    total = jnp.zeros((1, LANES), jnp.float32)
+    lane = lax.broadcasted_iota(jnp.int32, (1, LANES), 1)
+    for s, ref in enumerate(line_refs):
+        mine = jnp.where((lane // cols) % groups == s, ref[...], 0.0)
+        total = total + (mine if s == 0 else pltpu.roll(mine, LANES - s * cols, 1))
+    out_ref[...] = jnp.broadcast_to(total, out_ref.shape)
+
+
 def shifted(value, s, groups):
-    return lax.ppermute(value, "grp", [(i, (i + s) % groups) for i in range(groups)])
+    return lax.ppermute(value, "grp", [(i, i ^ s) for i in range(groups)])
 
 
 def in_hbm(value):
@@ -162,7 +174,7 @@
         compiler_params=grant(1),
         name="pack",
     )(in_hbm(tridiag_vectors.T), in_hbm(ritz_values[None, :]))
-    coefs = [own_coefs] + [shifted(own_coefs, groups - s, groups) for s in range(1, groups)]
+    coefs = [own_coefs] + [shifted(own_coefs, s, groups) for s in range(1, groups)]
 
     basis, image = krylov_basis, krylov_image
     turned = jax.ShapeDtypeStruct((outer, krylov, inner), krylov_basis.dtype)
@@ -175,7 +187,7 @@
     )(basis, image)
 
     chunk = (2 * cols * (outer + 1), LANES)
-    shapes = [(2 * cols, outer, LANES)] + [chunk] * (groups - 1) + [(members, LANES)]
+    shapes = [(2 * cols, outer, LANES)] + [chunk] * (groups - 1) + [(1, LANES)]
     outs = pl.pallas_call(
         functools.partial(project_kernel, groups=groups),
         out_shape=[jax.ShapeDtypeStruct(shape, f32) for shape in shapes],
@@ -184,16 +196,19 @@
         name="project",
     )(*coefs, basis, image)
     own, chunks, sums = outs[0], outs[1:groups], outs[groups]
-    sent = [shifted(c.astype(jnp.float16), s + 1, groups) for s, c in enumerate(chunks)]
+    sent = []
+    for s, c in enumerate(chunks):
+        sent.append(shifted(c.astype(jnp.float16), s + 1, groups))
     chunks = [c.astype(f32) for c in sent]
-    line = sums[:1]
+    line = sums
     moved = [line] + [shifted(line, s, groups) for s in range(1, groups)]
-    wide = lax.broadcasted_iota(jnp.int32, (1, LANES), 1)
-    total = jnp.zeros((1, LANES), f32)
-    for s, m in enumerate(moved):
-        here = (wide // cols) % groups == s
-        total = total + jnp.roll(jnp.where(here, m, 0.0), -s * cols, axis=1)
-    totals = lax.all_to_all(jnp.broadcast_to(total[None], (members, 1, LANES)), "row", split_axis=0, concat_axis=0, tiled=True, axis_index_groups=[[(r + LEADER) % members for r in range(members)]])
+    spread = pl.pallas_call(
+        functools.partial(total_kernel, cols=cols),
+        out_shape=jax.ShapeDtypeStruct((members, LANES), f32),
+        compiler_params=grant(1),
+        name="total",
+    )(*moved)
+    totals = lax.all_to_all(spread[:, None, :], "row", split_axis=0, concat_axis=0, tiled=True, axis_index_groups=[[(r + LEADER) % members for r in range(members)]])
     lines = [totals.sum(axis=0)]
     ritz, resid, norms = pl.pallas_call(
         functools.partial(finish_kernel, groups=groups, rows_total=rows_total),

time: 39.2 us -> 48.5 us (1.24)
  waiting for transfers between devices: 0.02 us -> 10.2 us
  starting transfers between devices: 11.2 us -> 10.2 us
    ppermute x9, waiting for transfers between devices: 0.02 us -> 10.2 us  [shifted(): return lax.ppermute(value, 'grp', [(i, i ^ s) for i in range(groups)])]
    ppermute x9, starting transfers between devices: 11.2 us -> 10.2 us  [shifted(): return lax.ppermute(value, 'grp', [(i, i ^ s) for i in range(groups)])]
  transfers between devices with their start and end apart: 9 -> 9, of which waited for: 0 -> 4; matrix products, arithmetic and copies ran while one was open for 1% -> 0% of each run, Pallas kernels for 8% -> 6%
where the time goes in v4:
time: 48.5 us; the launch traced here: 48.4 us
  blocking collectives  19.1 us (39%)
  starting transfers between devices  10.2 us (21%)
  waiting for transfers between devices  10.2 us (21%)
  Pallas kernels  7.77 us (16%)
  between operations  0.74 us (2%)
    all_to_all x1, blocking collectives, body(): lax.all_to_all(spread[:, None, :], 'row', split_axis=0, concat_axis=0, ti...  19.1 us
    ppermute x9, starting transfers between devices, shifted(): return lax.ppermute(value, 'grp', [(i, i ^ s) for i in range(groups)])  10.2 us
    ppermute x9, waiting for transfers between devices, shifted(): return lax.ppermute(value, 'grp', [(i, i ^ s) for i in range(groups)])  10.2 us
    pallas_call x1, Pallas kernels, body(): pl.pallas_call(stage_kernel, out_shape=[turned] * 2, cost_estimate=pl.Cos...  2.95 us
    pallas_call x1, Pallas kernels, body(): pl.pallas_call(functools.partial(project_kernel, groups=groups), out_shap...  2.2 us
    pallas_call x1, Pallas kernels, body(): pl.pallas_call(functools.partial(finish_kernel, groups=groups, rows_total...  1.6 us
  transfers between devices with their start and end apart: 9, of which 4 were waited for; matrix products, arithmetic and copies ran while one was open for 0% of the time, Pallas kernels for 6%

profile of v4, /device:TPU:1, one launch (start us, length us, event | category | flops | bytes accessed | tf_op | source)
XLA Modules:
  0.0 48.4 jit_solution(810938019570303755)
XLA Ops:
  0.7 0.9 %pack.1.refs_0_ = bf16[8,512]{1,0:T(8,128)(2,1)S(1)} custom-call(bf16[8,300]{1,0:T(8,128)(2,1)} %bitcast.9, bf16[1,8]{1,0:T(2,128)(2,1)} %bitcast.10), custom_call_target="tpu_custom_call" | custom-call | flops 6442450944 | bytes 16777216 | tf_op jit(solution)/shard_map/pack/pallas_call | solution.py:164
  1.6 3.4 %collective-permute-start.2 = (bf16[8,512]{1,0:T(8,128)(2,1)S(1)}, bf16[8,512]{1,0:T(8,128)(2,1)S(1)}, u32[]{:S(2)}, u32[]{:S(2)}) collective-permute-start(bf16[8,512]{1,0:T(8,128)(2,1)S(1)} %pack.1.refs_0_), channel_id=1, source_target_pairs={{0,192},{64,128},{128,64},{192,0},{1,193},{65,129},{129,65},{193,1... | collective-permute-start | bytes 24584 | tf_op jit(solution)/shard_map/ppermute | solution.py:145
  5.0 0.5 %collective-permute-start.1 = (bf16[8,512]{1,0:T(8,128)(2,1)S(1)}, bf16[8,512]{1,0:T(8,128)(2,1)S(1)}, u32[]{:S(2)}, u32[]{:S(2)}) collective-permute-start(bf16[8,512]{1,0:T(8,128)(2,1)S(1)} %pack.1.refs_0_), channel_id=1, source_target_pairs={{0,128},{64,192},{128,0},{192,64},{1,129},{65,193},{129,1},{193,65... | collective-permute-start | bytes 24584 | tf_op jit(solution)/shard_map/ppermute | solution.py:145
  5.5 0.2 collective-permute-start
  5.7 2.9 %stage.1 = (bf16[64,300,128]{2,1,0:T(8,128)(2,1)S(1)}, bf16[64,300,128]{2,1,0:T(8,128)(2,1)S(1)}) custom-call(bf16[300,64,128]{2,1,0:T(8,128)(2,1)S(1)} %copy-done, bf16[300,64,128]{2,1,0:T(8,128)(2,1)S(1)} %copy-done.1), custom_call_target="tpu_custom_call" | custom-call | flops 3221225472 | bytes 9830400 | tf_op jit(solution)/shard_map/stage/pallas_call | solution.py:181
  8.6 0.0 collective-permute-done.2.refs_3_
  8.6 0.4 collective-permute-done.1.refs_2_
  9.0 0.0 collective-permute-done.refs_1_
  9.0 2.2 %project.1 = (f32[16,64,128]{2,1,0:T(8,128)S(1)}, f32[1040,128]{1,0:T(8,128)S(1)}, f32[1040,128]{1,0:T(8,128)S(1)}, f32[1040,128]{1,0:T(8,128)S(1)}, f32[1,128]{1,0:T(1,128)S(1)}) custom-call(bf16[8,512]{1,0:T(8,128)(2,1)S(1)} %pack.1.refs_0_, bf16[8,512]{1,0:T(8,128)(2,1)S(1)} %collective-permute-done.refs_1_, ...), custom_call_target="tpu_custom_call" | custom-call | tf_op jit(solution)/shard_map/project/pallas_call | solution.py:191
  11.3 2.3 %collective-permute-start.5 = (f16[1040,128]{1,0:T(8,128)(2,1)S(1)}, f16[1040,128]{1,0:T(8,128)(2,1)S(1)}, u32[]{:S(2)}, u32[]{:S(2)}) collective-permute-start(f16[1040,128]{1,0:T(8,128)(2,1)S(1)} %convert_element_type.22), channel_id=1, source_target_pairs={{0,192},{64,128},{128,64},{192,0},{1,193},{65,129},{129,65},{193,1... | collective-permute-start | bytes 798728 | tf_op jit(solution)/shard_map/ppermute | solution.py:145
  13.6 0.5 %collective-permute-start.4 = (f16[1040,128]{1,0:T(8,128)(2,1)S(1)}, f16[1040,128]{1,0:T(8,128)(2,1)S(1)}, u32[]{:S(2)}, u32[]{:S(2)}) collective-permute-start(f16[1040,128]{1,0:T(8,128)(2,1)S(1)} %convert_element_type.20), channel_id=1, source_target_pairs={{0,128},{64,192},{128,0},{192,64},{1,129},{65,193},{129,1},{193,65... | collective-permute-start | bytes 798728 | tf_op jit(solution)/shard_map/ppermute | solution.py:145
  14.2 0.6 %collective-permute-start.3 = (f16[1040,128]{1,0:T(8,128)(2,1)S(1)}, f16[1040,128]{1,0:T(8,128)(2,1)S(1)}, u32[]{:S(2)}, u32[]{:S(2)}) collective-permute-start(f16[1040,128]{1,0:T(8,128)(2,1)S(1)} %convert_element_type.18), channel_id=1, source_target_pairs={{0,64},{64,0},{128,192},{192,128},{1,65},{65,1},{129,193},{193,129... | collective-permute-start | bytes 798728 | tf_op jit(solution)/shard_map/ppermute | solution.py:145
  14.8 2.2 %collective-permute-start.8 = (f32[1,128]{1,0:T(1,128)S(1)}, f32[1,128]{1,0:T(1,128)S(1)}, u32[]{:S(2)}, u32[]{:S(2)}) collective-permute-start(f32[1,128]{1,0:T(1,128)S(1)} %get-tuple-element.19.refs_0_), channel_id=1, source_target_pairs={{0,192},{64,128},{128,64},{192,0},{1,193},{65,129},{129,65},{193,1... | collective-permute-start | bytes 1544 | tf_op jit(solution)/shard_map/ppermute | solution.py:145
  17.0 0.5 %collective-permute-start.7 = (f32[1,128]{1,0:T(1,128)S(1)}, f32[1,128]{1,0:T(1,128)S(1)}, u32[]{:S(2)}, u32[]{:S(2)}) collective-permute-start(f32[1,128]{1,0:T(1,128)S(1)} %get-tuple-element.19.refs_0_), channel_id=1, source_target_pairs={{0,128},{64,192},{128,0},{192,64},{1,129},{65,193},{129,1},{193,65... | collective-permute-start | bytes 1544 | tf_op jit(solution)/shard_map/ppermute | solution.py:145
  17.5 7.1 %collective-permute-done.8.refs_3_ = f32[1,128]{1,0:T(1,128)S(1)} collective-permute-done((f32[1,128]{1,0:T(1,128)S(1)}, f32[1,128]{1,0:T(1,128)S(1)}, u32[]{:S(2)}, u32[]{:S(2)}) %collective-permute-start.8) | collective-permute-done | bytes 544 | tf_op jit(solution)/shard_map/ppermute | solution.py:145
  24.6 0.0 collective-permute-start.6
  24.6 1.9 %collective-permute-done.7.refs_2_ = f32[1,128]{1,0:T(1,128)S(1)} collective-permute-done((f32[1,128]{1,0:T(1,128)S(1)}, f32[1,128]{1,0:T(1,128)S(1)}, u32[]{:S(2)}, u32[]{:S(2)}) %collective-permute-start.7) | collective-permute-done | bytes 544 | tf_op jit(solution)/shard_map/ppermute | solution.py:145
  26.5 0.8 %collective-permute-done.6.refs_1_ = f32[1,128]{1,0:T(1,128)S(1)} collective-permute-done((f32[1,128]{1,0:T(1,128)S(1)}, f32[1,128]{1,0:T(1,128)S(1)}, u32[]{:S(2)}, u32[]{:S(2)}) %collective-permute-start.6) | collective-permute-done | bytes 544 | tf_op jit(solution)/shard_map/ppermute | solution.py:145
  27.3 0.1 total.1
  27.4 19.1 %all_to_all.5 = f32[64,1,128]{2,1,0:T(1,128)S(1)} all-to-all(f32[64,1,128]{2,1,0:T(1,128)S(1)} %bitcast.7), channel_id=1, replica_groups={{41,42,43,44,45,46,47,48,49,50,51,52,53,54,55,56,57,58,59,60,61,62,63,0..., dimensions={0} | all-to-all | bytes 65536 | tf_op jit(solution)/shard_map/all_to_all | solution.py:211
  46.5 0.1 reduce_sum.11
  46.6 0.0 collective-permute-done.5
  46.6 0.0 collective-permute-done.4
  46.8 1.6 %finish.1 = (f32[8,64,512]{2,1,0:T(8,128)}, f32[8,64,512]{2,1,0:T(8,128)}, f32[1,8]{1,0:T(1,128)}) custom-call(f32[16,64,128]{2,1,0:T(8,128)S(1)} %get-tuple-element.15.refs_0_, f32[1040,128]{1,0:T(8,128)S(1)} %convert_element_type.19.refs_1_, f32[1040,128]{1,0:T(8,128)S(1)} %convert_element_type.21.refs_2_, f32[1040,128]{1,0:T(8,128)S(1)} %convert_element_type.23.refs_3_, ...), custom_call_target="tpu_custom_call" | custom-call | tf_op jit(solution)/shard_map/finish/pallas_call | solution.py:213
  (11 shorter events, 0.2 us)
Async XLA Ops:
  0.6 5.0 %copy-start = (bf16[300,64,128]{2,1,0:T(8,128)(2,1)S(1)}, bf16[300,64,128]{2,1,0:T(8,128)(2,1)}, u32[]{:S(2)}) copy-start(bf16[300,64,128]{2,1,0:T(8,128)(2,1)} %basis_ref.1) | copy-start | bytes 14745604
  0.6 5.0 %copy-start.1 = (bf16[300,64,128]{2,1,0:T(8,128)(2,1)S(1)}, bf16[300,64,128]{2,1,0:T(8,128)(2,1)}, u32[]{:S(2)}) copy-start(bf16[300,64,128]{2,1,0:T(8,128)(2,1)} %image_ref.1) | copy-start | bytes 14745604
  1.6 7.0 %collective-permute-start.2 = (bf16[8,512]{1,0:T(8,128)(2,1)S(1)}, bf16[8,512]{1,0:T(8,128)(2,1)S(1)}, u32[]{:S(2)}, u32[]{:S(2)}) collective-permute-start(bf16[8,512]{1,0:T(8,128)(2,1)S(1)} %pack.1.refs_0_), channel_id=1, source_target_pairs={{0,192},{64,128},{128,64},{192,0},{1,193},{65,129},{129,65},{193,1... | collective-permute-start | bytes 24584 | tf_op jit(solution)/shard_map/ppermute | solution.py:145
  5.0 4.0 %collective-permute-start.1 = (bf16[8,512]{1,0:T(8,128)(2,1)S(1)}, bf16[8,512]{1,0:T(8,128)(2,1)S(1)}, u32[]{:S(2)}, u32[]{:S(2)}) collective-permute-start(bf16[8,512]{1,0:T(8,128)(2,1)S(1)} %pack.1.refs_0_), channel_id=1, source_target_pairs={{0,128},{64,192},{128,0},{192,64},{1,129},{65,193},{129,1},{193,65... | collective-permute-start | bytes 24584 | tf_op jit(solution)/shard_map/ppermute | solution.py:145
  5.5 3.5 %collective-permute-start = (bf16[8,512]{1,0:T(8,128)(2,1)S(1)}, bf16[8,512]{1,0:T(8,128)(2,1)S(1)}, u32[]{:S(2)}, u32[]{:S(2)}) collective-permute-start(bf16[8,512]{1,0:T(8,128)(2,1)S(1)} %pack.1.refs_0_), channel_id=1, source_target_pairs={{0,64},{64,0},{128,192},{192,128},{1,65},{65,1},{129,193},{193,129... | collective-permute-start | bytes 24584 | tf_op jit(solution)/shard_map/ppermute | solution.py:145
  11.3 35.3 %collective-permute-start.5 = (f16[1040,128]{1,0:T(8,128)(2,1)S(1)}, f16[1040,128]{1,0:T(8,128)(2,1)S(1)}, u32[]{:S(2)}, u32[]{:S(2)}) collective-permute-start(f16[1040,128]{1,0:T(8,128)(2,1)S(1)} %convert_element_type.22), channel_id=1, source_target_pairs={{0,192},{64,128},{128,64},{192,0},{1,193},{65,129},{129,65},{193,1... | collective-permute-start | bytes 798728 | tf_op jit(solution)/shard_map/ppermute | solution.py:145
  13.6 33.0 %collective-permute-start.4 = (f16[1040,128]{1,0:T(8,128)(2,1)S(1)}, f16[1040,128]{1,0:T(8,128)(2,1)S(1)}, u32[]{:S(2)}, u32[]{:S(2)}) collective-permute-start(f16[1040,128]{1,0:T(8,128)(2,1)S(1)} %convert_element_type.20), channel_id=1, source_target_pairs={{0,128},{64,192},{128,0},{192,64},{1,129},{65,193},{129,1},{193,65... | collective-permute-start | bytes 798728 | tf_op jit(solution)/shard_map/ppermute | solution.py:145
  14.2 32.5 %collective-permute-start.3 = (f16[1040,128]{1,0:T(8,128)(2,1)S(1)}, f16[1040,128]{1,0:T(8,128)(2,1)S(1)}, u32[]{:S(2)}, u32[]{:S(2)}) collective-permute-start(f16[1040,128]{1,0:T(8,128)(2,1)S(1)} %convert_element_type.18), channel_id=1, source_target_pairs={{0,64},{64,0},{128,192},{192,128},{1,65},{65,1},{129,193},{193,129... | collective-permute-start | bytes 798728 | tf_op jit(solution)/shard_map/ppermute | solution.py:145
  14.8 9.8 %collective-permute-start.8 = (f32[1,128]{1,0:T(1,128)S(1)}, f32[1,128]{1,0:T(1,128)S(1)}, u32[]{:S(2)}, u32[]{:S(2)}) collective-permute-start(f32[1,128]{1,0:T(1,128)S(1)} %get-tuple-element.19.refs_0_), channel_id=1, source_target_pairs={{0,192},{64,128},{128,64},{192,0},{1,193},{65,129},{129,65},{193,1... | collective-permute-start | bytes 1544 | tf_op jit(solution)/shard_map/ppermute | solution.py:145
  17.0 9.5 %collective-permute-start.7 = (f32[1,128]{1,0:T(1,128)S(1)}, f32[1,128]{1,0:T(1,128)S(1)}, u32[]{:S(2)}, u32[]{:S(2)}) collective-permute-start(f32[1,128]{1,0:T(1,128)S(1)} %get-tuple-element.19.refs_0_), channel_id=1, source_target_pairs={{0,128},{64,192},{128,0},{192,64},{1,129},{65,193},{129,1},{193,65... | collective-permute-start | bytes 1544 | tf_op jit(solution)/shard_map/ppermute | solution.py:145
  24.6 2.7 %collective-permute-start.6 = (f32[1,128]{1,0:T(1,128)S(1)}, f32[1,128]{1,0:T(1,128)S(1)}, u32[]{:S(2)}, u32[]{:S(2)}) collective-permute-start(f32[1,128]{1,0:T(1,128)S(1)} %get-tuple-element.19.refs_0_), channel_id=1, source_target_pairs={{0,64},{64,0},{128,192},{192,128},{1,65},{65,1},{129,193},{193,129... | collective-permute-start | bytes 1544 | tf_op jit(solution)/shard_map/ppermute | solution.py:145

commit v5 on v4

--- a/solution.py
+++ b/solution.py
@@ -98,36 +98,47 @@
                 ref[pl.ds(2 * cols * outer + which * cols, cols), :] = exponent[at : at + cols]
 
 
-def finish_kernel(*refs, groups, rows_total):
-    own_ref, chunk_refs, line_refs = refs[0], refs[1:groups], refs[groups:-3]
-    outs, norm_ref = refs[-3:-1], refs[-1]
+def assemble_kernel(*refs, groups):
+    own_ref, chunk_refs, outs = refs[0], refs[1:groups], refs[groups:]
     double, outer, _ = own_ref.shape
     cols = double // 2
-    row = lax.broadcasted_iota(jnp.int32, (cols, LANES), 0)
-    lane = lax.broadcasted_iota(jnp.int32, (cols, LANES), 1)
-    ritz, resid = jnp.zeros((cols, LANES), jnp.float32), jnp.zeros((cols, LANES), jnp.float32)
-    for s, ref in enumerate(line_refs):
-        ritz += jnp.where(lane == row + s * cols, ref[...], 0.0)
-        resid += jnp.where(lane == row + (s + groups) * cols, ref[...], 0.0)
-    ritz = jnp.sum(ritz, axis=1, keepdims=True) + 1.0
-    resid = jnp.sum(resid, axis=1, keepdims=True)
-    factor = jnp.broadcast_to(jnp.sqrt(rows_total / ritz), (cols, LANES))
-    norms = jnp.sqrt(resid / ritz)
-    norm_ref[...] = jnp.sum(jnp.where(lane == row, norms, 0.0), axis=0, keepdims=True)[:, :cols]
     me = lax.axis_index("grp")
     for s in range(groups):
         source = me ^ s
         at = pl.ds(pl.multiple_of(source * LANES, LANES), LANES)
         for which in range(2):
             if s == 0:
-                block = own_ref[which * cols : (which + 1) * cols]
-                gain = factor
+                outs[which][:, :, at] = own_ref[which * cols : (which + 1) * cols]
             else:
                 ref = chunk_refs[s - 1]
                 block = ref[pl.ds(which * cols * outer, cols * outer), :].reshape(cols, outer, LANES)
                 exponent = ref[pl.ds(2 * cols * outer + which * cols, cols), :]
-                gain = factor * power_of_two(exponent, -1)
-            outs[which][:, :, at] = block * gain[:, None, :]
+                outs[which][:, :, at] = block * power_of_two(exponent, -1)[:, None, :]
+
+
+def finish_kernel(ritz_ref, resid_ref, line_ref, ritz_out, resid_out, norm_out, held, norm_ref, sent, *, groups, rows_total, per_copy):
+    cols, _, inner = ritz_ref.shape
+    row = lax.broadcasted_iota(jnp.int32, (cols, LANES), 0)
+    lane = lax.broadcasted_iota(jnp.int32, (cols, LANES), 1)
+    line = line_ref[...]
+    ritz = jnp.sum(jnp.where(lane == row, line, 0.0), axis=1, keepdims=True) + 1.0
+    resid = jnp.sum(jnp.where(lane == row + groups * cols, line, 0.0), axis=1, keepdims=True)
+    factor = jnp.broadcast_to(jnp.sqrt(rows_total / ritz), (cols, LANES))
+    norms = jnp.sqrt(resid / ritz)
+    norm_ref[...] = jnp.sum(jnp.where(lane == row, norms, 0.0), axis=0, keepdims=True)[:, :cols]
+    copies = [pltpu.make_async_copy(norm_ref, norm_out, sent.at[0])]
+    copies[0].start()
+    for which, (ref, out) in enumerate(((ritz_ref, ritz_out), (resid_ref, resid_out))):
+        for i in range(0, cols, per_copy):
+            rows = pl.ds(i, per_copy)
+            for at in range(0, inner, LANES):
+                lanes = pl.ds(at, LANES)
+                held[which, rows, :, lanes] = ref[rows, :, lanes] * factor[i : i + per_copy][:, None, :]
+            copy = pltpu.make_async_copy(held.at[which, rows], out.at[rows], sent.at[len(copies)])
+            copy.start()
+            copies.append(copy)
+    for copy in copies:
+        copy.wait()
 
 
 def total_kernel(*refs, cols):
@@ -200,6 +211,13 @@
     for s, c in enumerate(chunks):
         sent.append(shifted(c.astype(jnp.float16), s + 1, groups))
     chunks = [c.astype(f32) for c in sent]
+    full = jax.ShapeDtypeStruct((cols, outer, groups * inner), f32)
+    ritz, resid = pl.pallas_call(
+        functools.partial(assemble_kernel, groups=groups),
+        out_shape=[full] * 2,
+        compiler_params=grant(4),
+        name="assemble",
+    )(own, *chunks)
     line = sums
     moved = [line] + [shifted(line, s, groups) for s in range(1, groups)]
     spread = pl.pallas_call(
@@ -211,12 +229,17 @@
     totals = lax.all_to_all(spread[:, None, :], "row", split_axis=0, concat_axis=0, tiled=True, axis_index_groups=[[(r + LEADER) % members for r in range(members)]])
     lines = [totals.sum(axis=0)]
     ritz, resid, norms = pl.pallas_call(
-        functools.partial(finish_kernel, groups=groups, rows_total=rows_total),
-        out_shape=[jax.ShapeDtypeStruct((cols, outer, groups * inner), f32)] * 2
-        + [jax.ShapeDtypeStruct((1, cols), f32)],
-        compiler_params=grant(12),
+        functools.partial(finish_kernel, groups=groups, rows_total=rows_total, per_copy=2),
+        out_specs=[pl.BlockSpec(memory_space=pltpu.HBM)] * 3,
+        out_shape=[full] * 2 + [jax.ShapeDtypeStruct((1, cols), f32)],
+        scratch_shapes=[
+            pltpu.VMEM((2, cols, outer, groups * inner), f32),
+            pltpu.VMEM((1, cols), f32),
+            pltpu.SemaphoreType.DMA((1 + 2 * cols // 2,)),
+        ],
+        compiler_params=grant(6),
         name="finish",
-    )(own, *chunks, *lines)
+    )(ritz, resid, *lines)
     return ritz, resid, norms.reshape(cols)
 
 

time: 48.5 us -> 48.7 us (level)
  no operation moved by 1% of the time
where the time goes in v5:
time: 48.7 us; the launch traced here: 48.6 us
  blocking collectives  19.1 us (39%)
  starting transfers between devices  10.2 us (21%)
  waiting for transfers between devices  10.2 us (21%)
  Pallas kernels  7.98 us (16%)
  between operations  0.75 us (2%)
    all_to_all x1, blocking collectives, body(): lax.all_to_all(spread[:, None, :], 'row', split_axis=0, concat_axis=0, ti...  19.1 us
    ppermute x9, starting transfers between devices, shifted(): return lax.ppermute(value, 'grp', [(i, i ^ s) for i in range(groups)])  10.2 us
    ppermute x9, waiting for transfers between devices, shifted(): return lax.ppermute(value, 'grp', [(i, i ^ s) for i in range(groups)])  10.2 us
    pallas_call x1, Pallas kernels, body(): pl.pallas_call(stage_kernel, out_shape=[turned] * 2, cost_estimate=pl.Cos...  2.95 us
    pallas_call x1, Pallas kernels, body(): pl.pallas_call(functools.partial(project_kernel, groups=groups), out_shap...  2.2 us
    pallas_call x1, Pallas kernels, body(): pl.pallas_call(functools.partial(finish_kernel, groups=groups, rows_total...  1.51 us
  transfers between devices with their start and end apart: 9, of which 4 were waited for; matrix products, arithmetic and copies ran while one was open for 0% of the time, Pallas kernels for 6%

profile of v5, /device:TPU:1, one launch (start us, length us, event | category | flops | bytes accessed | tf_op | source)
XLA Modules:
  0.0 48.6 jit_solution(3759662982144943059)
XLA Ops:
  0.7 0.9 %pack.1.refs_0_ = bf16[8,512]{1,0:T(8,128)(2,1)S(1)} custom-call(bf16[8,300]{1,0:T(8,128)(2,1)} %bitcast.9, bf16[1,8]{1,0:T(2,128)(2,1)} %bitcast.10), custom_call_target="tpu_custom_call" | custom-call | flops 6442450944 | bytes 16777216 | tf_op jit(solution)/shard_map/pack/pallas_call | solution.py:175
  1.6 3.4 %collective-permute-start.2 = (bf16[8,512]{1,0:T(8,128)(2,1)S(1)}, bf16[8,512]{1,0:T(8,128)(2,1)S(1)}, u32[]{:S(2)}, u32[]{:S(2)}) collective-permute-start(bf16[8,512]{1,0:T(8,128)(2,1)S(1)} %pack.1.refs_0_), channel_id=1, source_target_pairs={{0,192},{64,128},{128,64},{192,0},{1,193},{65,129},{129,65},{193,1... | collective-permute-start | bytes 24584 | tf_op jit(solution)/shard_map/ppermute | solution.py:156
  5.0 0.5 %collective-permute-start.1 = (bf16[8,512]{1,0:T(8,128)(2,1)S(1)}, bf16[8,512]{1,0:T(8,128)(2,1)S(1)}, u32[]{:S(2)}, u32[]{:S(2)}) collective-permute-start(bf16[8,512]{1,0:T(8,128)(2,1)S(1)} %pack.1.refs_0_), channel_id=1, source_target_pairs={{0,128},{64,192},{128,0},{192,64},{1,129},{65,193},{129,1},{193,65... | collective-permute-start | bytes 24584 | tf_op jit(solution)/shard_map/ppermute | solution.py:156
  5.5 0.2 collective-permute-start
  5.7 2.9 %stage.1 = (bf16[64,300,128]{2,1,0:T(8,128)(2,1)S(1)}, bf16[64,300,128]{2,1,0:T(8,128)(2,1)S(1)}) custom-call(bf16[300,64,128]{2,1,0:T(8,128)(2,1)S(1)} %copy-done, bf16[300,64,128]{2,1,0:T(8,128)(2,1)S(1)} %copy-done.1), custom_call_target="tpu_custom_call" | custom-call | flops 3221225472 | bytes 9830400 | tf_op jit(solution)/shard_map/stage/pallas_call | solution.py:192
  8.6 0.0 collective-permute-done.2.refs_3_
  8.6 0.4 collective-permute-done.1.refs_2_
  9.0 0.0 collective-permute-done.refs_1_
  9.0 2.2 %project.1 = (f32[16,64,128]{2,1,0:T(8,128)S(1)}, f32[1040,128]{1,0:T(8,128)S(1)}, f32[1040,128]{1,0:T(8,128)S(1)}, f32[1040,128]{1,0:T(8,128)S(1)}, f32[1,128]{1,0:T(1,128)S(1)}) custom-call(bf16[8,512]{1,0:T(8,128)(2,1)S(1)} %pack.1.refs_0_, bf16[8,512]{1,0:T(8,128)(2,1)S(1)} %collective-permute-done.refs_1_, ...), custom_call_target="tpu_custom_call" | custom-call | tf_op jit(solution)/shard_map/project/pallas_call | solution.py:202
  11.3 2.3 %collective-permute-start.5 = (f16[1040,128]{1,0:T(8,128)(2,1)S(1)}, f16[1040,128]{1,0:T(8,128)(2,1)S(1)}, u32[]{:S(2)}, u32[]{:S(2)}) collective-permute-start(f16[1040,128]{1,0:T(8,128)(2,1)S(1)} %convert_element_type.22), channel_id=1, source_target_pairs={{0,192},{64,128},{128,64},{192,0},{1,193},{65,129},{129,65},{193,1... | collective-permute-start | bytes 798728 | tf_op jit(solution)/shard_map/ppermute | solution.py:156
  13.6 0.5 %collective-permute-start.4 = (f16[1040,128]{1,0:T(8,128)(2,1)S(1)}, f16[1040,128]{1,0:T(8,128)(2,1)S(1)}, u32[]{:S(2)}, u32[]{:S(2)}) collective-permute-start(f16[1040,128]{1,0:T(8,128)(2,1)S(1)} %convert_element_type.20), channel_id=1, source_target_pairs={{0,128},{64,192},{128,0},{192,64},{1,129},{65,193},{129,1},{193,65... | collective-permute-start | bytes 798728 | tf_op jit(solution)/shard_map/ppermute | solution.py:156
  14.2 0.6 %collective-permute-start.3 = (f16[1040,128]{1,0:T(8,128)(2,1)S(1)}, f16[1040,128]{1,0:T(8,128)(2,1)S(1)}, u32[]{:S(2)}, u32[]{:S(2)}) collective-permute-start(f16[1040,128]{1,0:T(8,128)(2,1)S(1)} %convert_element_type.18), channel_id=1, source_target_pairs={{0,64},{64,0},{128,192},{192,128},{1,65},{65,1},{129,193},{193,129... | collective-permute-start | bytes 798728 | tf_op jit(solution)/shard_map/ppermute | solution.py:156
  14.8 2.2 %collective-permute-start.8 = (f32[1,128]{1,0:T(1,128)S(1)}, f32[1,128]{1,0:T(1,128)S(1)}, u32[]{:S(2)}, u32[]{:S(2)}) collective-permute-start(f32[1,128]{1,0:T(1,128)S(1)} %get-tuple-element.23.refs_0_), channel_id=1, source_target_pairs={{0,192},{64,128},{128,64},{192,0},{1,193},{65,129},{129,65},{193,1... | collective-permute-start | bytes 1544 | tf_op jit(solution)/shard_map/ppermute | solution.py:156
  17.0 0.5 %collective-permute-start.7 = (f32[1,128]{1,0:T(1,128)S(1)}, f32[1,128]{1,0:T(1,128)S(1)}, u32[]{:S(2)}, u32[]{:S(2)}) collective-permute-start(f32[1,128]{1,0:T(1,128)S(1)} %get-tuple-element.23.refs_0_), channel_id=1, source_target_pairs={{0,128},{64,192},{128,0},{192,64},{1,129},{65,193},{129,1},{193,65... | collective-permute-start | bytes 1544 | tf_op jit(solution)/shard_map/ppermute | solution.py:156
  17.5 7.1 %collective-permute-done.8.refs_3_ = f32[1,128]{1,0:T(1,128)S(1)} collective-permute-done((f32[1,128]{1,0:T(1,128)S(1)}, f32[1,128]{1,0:T(1,128)S(1)}, u32[]{:S(2)}, u32[]{:S(2)}) %collective-permute-start.8) | collective-permute-done | bytes 544 | tf_op jit(solution)/shard_map/ppermute | solution.py:156
  24.6 0.0 collective-permute-start.6
  24.6 1.9 %collective-permute-done.7.refs_2_ = f32[1,128]{1,0:T(1,128)S(1)} collective-permute-done((f32[1,128]{1,0:T(1,128)S(1)}, f32[1,128]{1,0:T(1,128)S(1)}, u32[]{:S(2)}, u32[]{:S(2)}) %collective-permute-start.7) | collective-permute-done | bytes 544 | tf_op jit(solution)/shard_map/ppermute | solution.py:156
  26.5 0.8 %collective-permute-done.6.refs_1_ = f32[1,128]{1,0:T(1,128)S(1)} collective-permute-done((f32[1,128]{1,0:T(1,128)S(1)}, f32[1,128]{1,0:T(1,128)S(1)}, u32[]{:S(2)}, u32[]{:S(2)}) %collective-permute-start.6) | collective-permute-done | bytes 544 | tf_op jit(solution)/shard_map/ppermute | solution.py:156
  27.3 0.1 total.1
  27.4 19.1 %all_to_all.5 = f32[64,1,128]{2,1,0:T(1,128)S(1)} all-to-all(f32[64,1,128]{2,1,0:T(1,128)S(1)} %bitcast.7), channel_id=1, replica_groups={{41,42,43,44,45,46,47,48,49,50,51,52,53,54,55,56,57,58,59,60,61,62,63,0..., dimensions={0} | all-to-all | bytes 65536 | tf_op jit(solution)/shard_map/all_to_all | solution.py:229
  46.5 0.1 reduce_sum.11
  46.6 0.0 collective-permute-done.4
  46.8 0.3 assemble.1
  47.1 1.5 %finish.1 = (f32[8,64,512]{2,1,0:T(8,128)}, f32[8,64,512]{2,1,0:T(8,128)}, f32[1,8]{1,0:T(1,128)}) custom-call(f32[8,64,512]{2,1,0:T(8,128)S(1)} %get-tuple-element.21.ritz_ref, f32[8,64,512]{2,1,0:T(8,128)S(1)} %get-tuple-element.22.resid_ref, f32[1,128]{1,0:T(1,128)S(1)} %bitcast.8), custom_call_target="tpu_custom_call" | custom-call | tf_op jit(solution)/shard_map/finish/pallas_call | solution.py:231
  (12 shorter events, 0.2 us)
Async XLA Ops:
  0.6 5.0 %copy-start = (bf16[300,64,128]{2,1,0:T(8,128)(2,1)S(1)}, bf16[300,64,128]{2,1,0:T(8,128)(2,1)}, u32[]{:S(2)}) copy-start(bf16[300,64,128]{2,1,0:T(8,128)(2,1)} %basis_ref.1) | copy-start | bytes 14745604
  0.6 5.0 %copy-start.1 = (bf16[300,64,128]{2,1,0:T(8,128)(2,1)S(1)}, bf16[300,64,128]{2,1,0:T(8,128)(2,1)}, u32[]{:S(2)}) copy-start(bf16[300,64,128]{2,1,0:T(8,128)(2,1)} %image_ref.1) | copy-start | bytes 14745604
  1.6 7.0 %collective-permute-start.2 = (bf16[8,512]{1,0:T(8,128)(2,1)S(1)}, bf16[8,512]{1,0:T(8,128)(2,1)S(1)}, u32[]{:S(2)}, u32[]{:S(2)}) collective-permute-start(bf16[8,512]{1,0:T(8,128)(2,1)S(1)} %pack.1.refs_0_), channel_id=1, source_target_pairs={{0,192},{64,128},{128,64},{192,0},{1,193},{65,129},{129,65},{193,1... | collective-permute-start | bytes 24584 | tf_op jit(solution)/shard_map/ppermute | solution.py:156
  5.0 4.0 %collective-permute-start.1 = (bf16[8,512]{1,0:T(8,128)(2,1)S(1)}, bf16[8,512]{1,0:T(8,128)(2,1)S(1)}, u32[]{:S(2)}, u32[]{:S(2)}) collective-permute-start(bf16[8,512]{1,0:T(8,128)(2,1)S(1)} %pack.1.refs_0_), channel_id=1, source_target_pairs={{0,128},{64,192},{128,0},{192,64},{1,129},{65,193},{129,1},{193,65... | collective-permute-start | bytes 24584 | tf_op jit(solution)/shard_map/ppermute | solution.py:156
  5.5 3.5 %collective-permute-start = (bf16[8,512]{1,0:T(8,128)(2,1)S(1)}, bf16[8,512]{1,0:T(8,128)(2,1)S(1)}, u32[]{:S(2)}, u32[]{:S(2)}) collective-permute-start(bf16[8,512]{1,0:T(8,128)(2,1)S(1)} %pack.1.refs_0_), channel_id=1, source_target_pairs={{0,64},{64,0},{128,192},{192,128},{1,65},{65,1},{129,193},{193,129... | collective-permute-start | bytes 24584 | tf_op jit(solution)/shard_map/ppermute | solution.py:156
  11.3 35.3 %collective-permute-start.5 = (f16[1040,128]{1,0:T(8,128)(2,1)S(1)}, f16[1040,128]{1,0:T(8,128)(2,1)S(1)}, u32[]{:S(2)}, u32[]{:S(2)}) collective-permute-start(f16[1040,128]{1,0:T(8,128)(2,1)S(1)} %convert_element_type.22), channel_id=1, source_target_pairs={{0,192},{64,128},{128,64},{192,0},{1,193},{65,129},{129,65},{193,1... | collective-permute-start | bytes 798728 | tf_op jit(solution)/shard_map/ppermute | solution.py:156
  13.6 33.0 %collective-permute-start.4 = (f16[1040,128]{1,0:T(8,128)(2,1)S(1)}, f16[1040,128]{1,0:T(8,128)(2,1)S(1)}, u32[]{:S(2)}, u32[]{:S(2)}) collective-permute-start(f16[1040,128]{1,0:T(8,128)(2,1)S(1)} %convert_element_type.20), channel_id=1, source_target_pairs={{0,128},{64,192},{128,0},{192,64},{1,129},{65,193},{129,1},{193,65... | collective-permute-start | bytes 798728 | tf_op jit(solution)/shard_map/ppermute | solution.py:156
  14.2 32.5 %collective-permute-start.3 = (f16[1040,128]{1,0:T(8,128)(2,1)S(1)}, f16[1040,128]{1,0:T(8,128)(2,1)S(1)}, u32[]{:S(2)}, u32[]{:S(2)}) collective-permute-start(f16[1040,128]{1,0:T(8,128)(2,1)S(1)} %convert_element_type.18), channel_id=1, source_target_pairs={{0,64},{64,0},{128,192},{192,128},{1,65},{65,1},{129,193},{193,129... | collective-permute-start | bytes 798728 | tf_op jit(solution)/shard_map/ppermute | solution.py:156
  14.8 9.8 %collective-permute-start.8 = (f32[1,128]{1,0:T(1,128)S(1)}, f32[1,128]{1,0:T(1,128)S(1)}, u32[]{:S(2)}, u32[]{:S(2)}) collective-permute-start(f32[1,128]{1,0:T(1,128)S(1)} %get-tuple-element.23.refs_0_), channel_id=1, source_target_pairs={{0,192},{64,128},{128,64},{192,0},{1,193},{65,129},{129,65},{193,1... | collective-permute-start | bytes 1544 | tf_op jit(solution)/shard_map/ppermute | solution.py:156
  17.0 9.5 %collective-permute-start.7 = (f32[1,128]{1,0:T(1,128)S(1)}, f32[1,128]{1,0:T(1,128)S(1)}, u32[]{:S(2)}, u32[]{:S(2)}) collective-permute-start(f32[1,128]{1,0:T(1,128)S(1)} %get-tuple-element.23.refs_0_), channel_id=1, source_target_pairs={{0,128},{64,192},{128,0},{192,64},{1,129},{65,193},{129,1},{193,65... | collective-permute-start | bytes 1544 | tf_op jit(solution)/shard_map/ppermute | solution.py:156
  24.6 2.7 %collective-permute-start.6 = (f32[1,128]{1,0:T(1,128)S(1)}, f32[1,128]{1,0:T(1,128)S(1)}, u32[]{:S(2)}, u32[]{:S(2)}) collective-permute-start(f32[1,128]{1,0:T(1,128)S(1)} %get-tuple-element.23.refs_0_), channel_id=1, source_target_pairs={{0,64},{64,0},{128,192},{192,128},{1,65},{65,1},{129,193},{193,129... | collective-permute-start | bytes 1544 | tf_op jit(solution)/shard_map/ppermute | solution.py:156
